TPU v7x, 128 devices: a whole 4x4x4 slice. The times are simulated.
128 devices in a mesh: dom: 128 (over z, x, y, core).
Axes of the slice: x: 4, y: 4, z: 4, core: 2. Of those that a mesh axis runs over, the one named last changes fastest.
Arguments:
- field: float32 [3, 720896], P(None, 'dom'), may hold values from -6 to 6
- blocks: bfloat16 [30, 30, 524288], P(None, None, 'dom'), may hold values from -1 to 1
- connectivity: int32 [10, 524288], P(None, 'dom'), may hold values from 0 to 8703, as said below
- send_nodes: int32 [8, 49152], P(None, 'dom'), may hold values from 0 to 5631
- live_blocks: int32 [128], replicated, may hold values from 1 to 8
Outputs:
- image: float32 [3, 720896], P(None, 'dom')
Inputs may be any that keep to these rules, and one draw needn't show every extreme that they name: `connectivity`: entries below 5632 name nodes of the element's own subdomain; entry 5632 + k * 384 + g names the node sent as entry g of row k by subdomain d - o_k, and only where that subdomain exists. `send_nodes`: columns d * 384 to (d + 1) * 384 - 1 of row k list local indices of nodes that subdomain d owns, in the order in which subdomain d + o_k numbers its ghost slots from d. Subdomain d's elements fill its first 512 * live_blocks[d] slots; the other slots are unused.
All inputs are finite; a program needn't handle non-finite values.
Results may differ from a plain program's by a relative error of at most 0.0003.
Values sent between devices are 32-bit elements; how exact they have to be, the bound alone decides.
No kernel may reach another device: no remote copies, remote signals or barrier semaphores. Data moves between devices by JAX's collectives and lax.ppermute only.
A program may use at most 64 MiB of HBM per device.

v0:
```python
import jax
import jax.numpy as jnp
from jax import lax
from jax.experimental import pallas as pl
from jax.experimental.pallas import tpu as pltpu
from jax.sharding import PartitionSpec as P

F32 = jnp.float32
BF16 = jnp.bfloat16
LANES = 128
WIDE = 256
BLK = 512
ELEMS = 4096
NBLK = ELEMS // BLK
NODES = 5632
GHOST = 384
SLOTS = NODES + 8 * GHOST
OWN_ROWS = NODES // WIDE
ALL_ROWS = SLOTS // WIDE
TILES = BLK // LANES
VMEM = pl.BlockSpec(memory_space=pltpu.VMEM)
HBM = pl.BlockSpec(memory_space=pltpu.HBM)


def pad16(n):
    return -(-n // 16) * 16


def iota_rows(rows):
    return lax.broadcasted_iota(jnp.int32, (rows, LANES), 0)


def row_upper(rows, first, count):
    q = iota_rows(count) + first
    u = q
    for s in range(1, 6):
        u = jnp.where(q >= s * rows, q - s * rows, u)
    return jnp.where(q >= 6 * rows, -1, u).astype(F32)


def lower_parts():
    return [(iota_rows(16) + 16 * g).astype(F32).astype(BF16) for g in range(WIDE // 16)]


def upper_parts(rows):
    return [row_upper(rows, 16 * g, 16).astype(BF16) for g in range(pad16(6 * rows) // 16)]


def wide(row):
    return jnp.broadcast_to(row, (16, LANES)).astype(BF16)


def one_hot(parts, row):
    here, one, zero = wide(row), jnp.ones((16, LANES), BF16), jnp.zeros((16, LANES), BF16)
    return jnp.concatenate([jnp.where(part == here, one, zero) for part in parts], axis=0)


def split(x):
    hi = x.astype(BF16).astype(F32)
    return hi, x - hi


def placed(uppers, row, values, rows):
    here, zero = wide(row), jnp.zeros((16, LANES), BF16)
    values = [wide(v) for v in values]
    out = []
    for g, upper in enumerate(uppers):
        first, last = 16 * g // rows, (16 * g + 15) // rows
        value = values[min(first, 5)]
        if last != first and last <= 5:
            cut = (first + 1) * rows - 16 * g
            head = iota_rows(16).astype(F32).astype(BF16) < jnp.full((16, LANES), cut, BF16)
            value = jnp.where(head, value, values[last])
        out.append(jnp.where(upper == here, value, zero))
    return jnp.concatenate(out, axis=0)


def side():
    return lax.rem(lax.axis_index("dom"), 2)


def by_label(x):
    return jnp.where(side() == 1, pltpu.roll(x, 4, axis=0), x)


def pick_kernel(field_hbm, send_hbm, swap_ref, out_ref, field_ref, send_ref, sem):
    copies = [pltpu.make_async_copy(field_hbm, field_ref, sem.at[0]), pltpu.make_async_copy(send_hbm, send_ref, sem.at[1])]
    for copy in copies:
        copy.start()
    for copy in copies:
        copy.wait()
    place = {0: (swap_ref, 0), 4: (swap_ref, 9), 5: (swap_ref, 18), 6: (swap_ref, 27), 7: (swap_ref, 36),
             1: (out_ref, 0), 2: (out_ref, 9), 3: (out_ref, 18)}
    for j in range(3):
        index = by_label(send_ref[:, pl.ds(j * LANES, LANES)])
        upper, lower = index >> 7, index & 127
        total = [jnp.zeros((8, LANES), F32) for _ in range(3)]
        for h in range(NODES // LANES):
            hit = upper == h
            for c in range(3):
                row = jnp.broadcast_to(field_ref[pl.ds(c, 1), pl.ds(h * LANES, LANES)], (8, LANES))
                total[c] = jnp.where(hit, jnp.take_along_axis(row, lower, axis=1), total[c])
        for c in range(3):
            for m in range(8):
                ref, base = place[m]
                ref[pl.ds(base + c * 3 + j, 1), :] = total[c][m:m + 1, :]


def main_kernel(live_ref, field_hbm, near_ref, one_ref, two_ref, last_ref, conn_hbm, blocks_ref,
                own_ref, swap_ref, one_out_ref, two_out_ref,
                field_ref, conn_ref, early, stiff, sem, tf, lo, up, vals, high, low, total):
    n = live_ref[lax.axis_index("dom")]
    second = side() == 1
    field_copy = pltpu.make_async_copy(field_hbm, field_ref, early.at[0])
    conn_copy = pltpu.make_async_copy(conn_hbm, conn_ref, early.at[1])
    field_copy.start()
    conn_copy.start()

    def fetch(b):
        cols = pl.ds(pl.multiple_of(b * BLK, BLK), BLK)
        return pltpu.make_async_copy(blocks_ref.at[:, :, cols], stiff.at[b], sem.at[b])

    def start(b, _):
        fetch(b).start()
        return 0

    lax.fori_loop(0, n, start, 0)

    tf[pl.ds(200, 8), :] = jnp.zeros((8, WIDE), F32)

    def fill(x, c, h):
        hi, low = split(x)
        for part, y in ((0, hi), (1, low)):
            tf[pl.ds((c * 2 + part) * ALL_ROWS + h // 2, 1), pl.ds((h % 2) * LANES, LANES)] = y

    field_copy.wait()
    for h in range(NODES // LANES):
        x = field_ref[:, pl.ds(h * LANES, LANES)]
        for c in range(3):
            fill(x[c:c + 1, :], c, h)
    source = {0: (one_ref, 9), 1: (one_ref, 0), 2: (two_ref, 9), 3: (two_ref, 0),
              4: (near_ref, 0), 5: (last_ref, 9), 6: (last_ref, 0), 7: (last_ref, 18)}
    ghost = [source[m][0][pl.ds(source[m][1], 9), :] for m in range(8)]
    for k in range(8):
        bundle = jnp.where(second, ghost[k ^ 4], ghost[k])
        for c in range(3):
            for j in range(3):
                q = c * 3 + j
                fill(bundle[q:q + 1, :], c, NODES // LANES + 3 * k + j)
    table = tf[...].astype(BF16)
    lowers, uppers = lower_parts(), upper_parts(ALL_ROWS)
    per = 2 * ALL_ROWS
    even = [row_upper(ALL_ROWS, 8 * g, 8) for g in range(9)]
    odd = [row_upper(ALL_ROWS, 8 * g, 8) for g in range(8, 17)]
    head = iota_rows(8) < per % 8
    even[8] = jnp.where(head, even[8], -1.0)
    odd[0] = jnp.where(head, -1.0, odd[0])
    total[...] = jnp.zeros_like(total)
    conn_copy.wait()

    def step(b, _):
        index = conn_ref[:, pl.ds(pl.multiple_of(b * BLK, BLK), BLK)]
        lo[...] = (index & (WIDE - 1)).astype(F32)
        up[...] = (index >> 8).astype(F32)
        for a in range(10):
            for t2 in range(TILES // 2):
                cols = [pl.ds((2 * t2 + s) * LANES, LANES) for s in range(2)]
                hot = jnp.concatenate([one_hot(lowers, lo[pl.ds(a, 1), c]) for c in cols], axis=1)
                got = jnp.dot(table, hot, preferred_element_type=F32)
                for s in range(2):
                    here = jnp.broadcast_to(up[pl.ds(a, 1), cols[s]], (8, LANES))
                    sums = [jnp.zeros((8, LANES), F32)] * 3
                    for g in range(9):
                        hit = even[g] == here
                        for c in (0, 2):
                            q = 8 * g + c * per
                            sums[c] = jnp.where(hit, got[q:q + 8, s * LANES:(s + 1) * LANES], sums[c])
                        q = 64 + 8 * g
                        sums[1] = jnp.where(odd[g] == here, got[q:q + 8, s * LANES:(s + 1) * LANES], sums[1])
                    for c in range(3):
                        vals[pl.ds(c * 10 + a, 1), cols[s]] = jnp.sum(sums[c], axis=0, keepdims=True)
        fetch(b).wait()
        for t in range(TILES):
            cols = pl.ds(t * LANES, LANES)
            v = vals[:, cols]
            for i in range(30):
                k = stiff[b, i, :, cols].astype(F32)
                high[pl.ds(i, 1), cols] = jnp.sum(k * v, axis=0, keepdims=True)
        high[...], low[...] = split(high[...])
        acc = None
        for a in range(10):
            for t2 in range(TILES // 2):
                hot, put = [], []
                for s in range(2):
                    cols = pl.ds((2 * t2 + s) * LANES, LANES)
                    hot.append(one_hot(lowers, lo[pl.ds(a, 1), cols]))
                    values = [ref[pl.ds(c * 10 + a, 1), cols] for c in range(3) for ref in (high, low)]
                    put.append(placed(uppers, up[pl.ds(a, 1), cols], values, ALL_ROWS))
                part = lax.dot_general(jnp.concatenate(put, axis=1), jnp.concatenate(hot, axis=1), (((1,), (1,)), ((), ())),
                                       preferred_element_type=F32)
                acc = part if acc is None else acc + part
        total[...] += acc
        return 0

    lax.fori_loop(0, n, step, 0)

    for c in range(3):
        base = 2 * c * ALL_ROWS
        own_ref[pl.ds(c * OWN_ROWS, OWN_ROWS), :] = total[pl.ds(base, OWN_ROWS), :] + total[pl.ds(base + ALL_ROWS, OWN_ROWS), :]
    target = {6: (swap_ref, 0), 5: (swap_ref, 9), 7: (swap_ref, 18), 4: (swap_ref, 27),
              1: (one_out_ref, 0), 0: (one_out_ref, 9), 3: (two_out_ref, 0), 2: (two_out_ref, 9)}

    def partial(k, c, j):
        h = NODES // LANES + 3 * k + j
        at = 2 * c * ALL_ROWS + h // 2
        cols = pl.ds((h % 2) * LANES, LANES)
        return total[pl.ds(at, 1), cols] + total[pl.ds(at + ALL_ROWS, 1), cols]

    for m in range(4):
        for c in range(3):
            for j in range(3):
                low, high = partial(m, c, j), partial(m + 4, c, j)
                for label, x in ((m, jnp.where(second, high, low)), (m + 4, jnp.where(second, low, high))):
                    ref, base = target[label]
                    ref[pl.ds(base + c * 3 + j, 1), :] = x


def spread_kernel(own_ref, swap_ref, one_ref, two_ref, last_ref, send_ref, out_ref, lo, up):
    lowers, uppers = lower_parts(), upper_parts(OWN_ROWS)
    index = by_label(send_ref[...])
    lo[...] = (index & (WIDE - 1)).astype(F32)
    up[...] = (index >> 8).astype(F32)
    source = {0: (swap_ref, 27), 1: (one_ref, 0), 2: (one_ref, 18), 3: (two_ref, 0),
              4: (last_ref, 0), 5: (last_ref, 9), 6: (last_ref, 18), 7: (last_ref, 27)}
    hot, put = [], []
    for m in range(8):
        ref, base = source[m]
        for j in range(3):
            cols = pl.ds(j * LANES, LANES)
            hot.append(one_hot(lowers, lo[pl.ds(m, 1), cols]))
            values = [x for c in range(3) for x in split(ref[pl.ds(base + c * 3 + j, 1), :])]
            put.append(placed(uppers, up[pl.ds(m, 1), cols], values, OWN_ROWS))
    total = None
    for g in range(0, 24, 2):
        part = lax.dot_general(jnp.concatenate(put[g:g + 2], axis=1), jnp.concatenate(hot[g:g + 2], axis=1),
                               (((1,), (1,)), ((), ())), preferred_element_type=F32)
        total = part if total is None else total + part
    for c in range(3):
        for u in range(OWN_ROWS):
            q = 2 * c * OWN_ROWS + u
            out_ref[pl.ds(c, 1), pl.ds(u * WIDE, WIDE)] = (
                total[q:q + 1, :] + total[q + OWN_ROWS:q + OWN_ROWS + 1, :] + own_ref[pl.ds(c * OWN_ROWS + u, 1), :]
            )


def across(x):
    return lax.ppermute(x, "dom", [(i, i ^ 1) for i in range(lax.axis_size("dom"))])


def along(x, o):
    n = lax.axis_size("dom")
    route = {i: i + (2 * o if i % 2 == 0 else -2 * o) for i in range(n)}
    spare = sorted(set(range(n)) - set(route.values()))
    for i in range(n):
        if route[i] not in range(n):
            route[i] = min(spare, key=lambda j: (abs(j - i), j))
            spare.remove(route[i])
    return lax.ppermute(x, "dom", list(route.items()))


def in_hbm(x):
    return pltpu.with_memory_space_constraint(x, pltpu.HBM)


def params(kib):
    return pltpu.CompilerParams(vmem_limit_bytes=kib * 1024)


def body(field, blocks, connectivity, send_nodes, live_blocks):
    f = lambda *s: jax.ShapeDtypeStruct(s, F32)
    swap, out = pl.pallas_call(
        pick_kernel, out_shape=(f(45, LANES), f(27, LANES)), in_specs=[HBM] * 2, out_specs=(VMEM,) * 2,
        scratch_shapes=[pltpu.VMEM((3, NODES), F32), pltpu.VMEM((8, GHOST), jnp.int32), pltpu.SemaphoreType.DMA((2,))],
        compiler_params=params(1024), name="pick",
    )(in_hbm(field), in_hbm(send_nodes))
    near = across(swap)
    one = along(jnp.concatenate([out[:9], near[9:18], out[9:18], near[18:27]]), 1)
    two = along(jnp.concatenate([out[18:], near[27:]]), 2)
    last = across(jnp.concatenate([one[18:], two[18:]]))
    rows = pad16(6 * ALL_ROWS)
    own, swap, one_out, two_out = pl.pallas_call(
        main_kernel,
        out_shape=(f(3 * OWN_ROWS, WIDE), f(36, LANES), f(18, LANES), f(18, LANES)),
        in_specs=[pl.BlockSpec(memory_space=pltpu.SMEM), HBM] + [VMEM] * 4 + [HBM] * 2,
        out_specs=(VMEM,) * 4,
        scratch_shapes=[
            pltpu.VMEM((3, NODES), F32),
            pltpu.VMEM((10, ELEMS), jnp.int32),
            pltpu.SemaphoreType.DMA((2,)),
            pltpu.VMEM((NBLK, 30, 30, BLK), BF16),
            pltpu.SemaphoreType.DMA((NBLK,)),
            pltpu.VMEM((rows, WIDE), F32),
            pltpu.VMEM((10, BLK), F32),
            pltpu.VMEM((10, BLK), F32),
            pltpu.VMEM((30, BLK), F32),
            pltpu.VMEM((30, BLK), F32),
            pltpu.VMEM((30, BLK), F32),
            pltpu.VMEM((rows, WIDE), F32),
        ],
        compiler_params=params(32768),
        name="main",
    )(in_hbm(live_blocks), in_hbm(field), near, one, two, last, in_hbm(connectivity), in_hbm(blocks))
    swapped = across(swap)
    one_in = along(jnp.concatenate([one_out, swapped[:18]]), -1)
    two_in = along(jnp.concatenate([two_out, swapped[18:27]]), -2)
    back = across(jnp.concatenate([one_in[9:18], one_in[27:], two_in[9:]]))
    return pl.pallas_call(
        spread_kernel,
        out_shape=f(3, NODES),
        in_specs=[VMEM] * 6,
        out_specs=VMEM,
        scratch_shapes=[
            pltpu.VMEM((8, GHOST), F32),
            pltpu.VMEM((8, GHOST), F32),
        ],
        compiler_params=params(8192),
        name="spread",
    )(own, swapped, one_in, two_in, back, send_nodes)


def solution(mesh):
    return jax.shard_map(
        body,
        mesh=mesh,
        in_specs=(P(None, "dom"), P(None, None, "dom"), P(None, "dom"), P(None, "dom"), P()),
        out_specs=P(None, "dom"),
        check_vma=False,
    )
```

profile of v0, /device:TPU:65, one launch (start us, length us, event | category | flops | bytes accessed | tf_op | source)
XLA Modules:
  0.0 43.0 jit_solution(2629548567189747236)
XLA Ops:
  0.0 0.0 copy-start
  0.0 1.4 %pick.1 = (f32[45,128]{1,0:T(8,128)S(1)}, f32[27,128]{1,0:T(8,128)S(1)}) custom-call(f32[3,5632]{1,0:T(4,128)} %field_hbm.3, s32[8,384]{1,0:T(8,128)} %send_ref.1), custom_call_target="tpu_custom_call" | custom-call | tf_op jit(solution)/shard_map/pick/pallas_call | solution.py:281
  1.4 0.8 %collective-permute-start = (f32[45,128]{1,0:T(8,128)S(1)}, f32[45,128]{1,0:T(8,128)S(1)}, u32[]{:S(2)}, u32[]{:S(2)}) collective-permute-start(f32[45,128]{1,0:T(8,128)S(1)} %get-tuple-element.11), channel_id=1, source_target_pairs={{0,1},{1,0},{2,3},{3,2},{4,5},{5,4},{6,7},{7,6},{8,9},{9,8},{10,11... | collective-permute-start | bytes 69128 | tf_op jit(solution)/shard_map/ppermute | solution.py:257
  2.2 0.8 %collective-permute-done.near_ref = f32[45,128]{1,0:T(8,128)S(1)} collective-permute-done((f32[45,128]{1,0:T(8,128)S(1)}, f32[45,128]{1,0:T(8,128)S(1)}, u32[]{:S(2)}, u32[]{:S(2)}) %collective-permute-start) | collective-permute-done | bytes 23072 | tf_op jit(solution)/shard_map/ppermute | solution.py:257
  3.1 4.5 %collective-permute-start.1 = (f32[36,128]{1,0:T(8,128)S(1)}, f32[36,128]{1,0:T(8,128)S(1)}, u32[]{:S(2)}, u32[]{:S(2)}) collective-permute-start(f32[36,128]{1,0:T(8,128)S(1)} %pad_maximum_fusion), channel_id=1, source_target_pairs={{0,2},{1,0},{2,4},{3,1},{4,6},{5,3},{6,8},{7,5},{8,10},{9,7},{10,1... | collective-permute-start | bytes 55304 | tf_op jit(solution)/shard_map/ppermute | solution.py:268
  7.6 0.4 collective-permute-start.2
  8.0 4.0 %collective-permute-done.2.two_ref = f32[27,128]{1,0:T(8,128)S(1)} collective-permute-done((f32[27,128]{1,0:T(8,128)S(1)}, f32[27,128]{1,0:T(8,128)S(1)}, u32[]{:S(2)}, u32[]{:S(2)}) %collective-permute-start.2) | collective-permute-done | bytes 13856 | tf_op jit(solution)/shard_map/ppermute | solution.py:268
  12.1 0.0 collective-permute-done.1.one_ref
  12.1 1.4 %collective-permute-start.3 = (f32[27,128]{1,0:T(8,128)S(1)}, f32[27,128]{1,0:T(8,128)S(1)}, u32[]{:S(2)}, u32[]{:S(2)}) collective-permute-start(f32[27,128]{1,0:T(8,128)S(1)} %pad_maximum_fusion.4), channel_id=1, source_target_pairs={{0,1},{1,0},{2,3},{3,2},{4,5},{5,4},{6,7},{7,6},{8,9},{9,8},{10,11... | collective-permute-start | bytes 41480 | tf_op jit(solution)/shard_map/ppermute | solution.py:257
  13.5 0.8 %collective-permute-done.3.last_ref = f32[27,128]{1,0:T(8,128)S(1)} collective-permute-done((f32[27,128]{1,0:T(8,128)S(1)}, f32[27,128]{1,0:T(8,128)S(1)}, u32[]{:S(2)}, u32[]{:S(2)}) %collective-permute-start.3) | collective-permute-done | bytes 13856 | tf_op jit(solution)/shard_map/ppermute | solution.py:257
  14.3 12.1 %main.1 = (f32[66,256]{1,0:T(8,128)S(1)}, f32[36,128]{1,0:T(8,128)S(1)}, f32[18,128]{1,0:T(8,128)S(1)}, f32[18,128]{1,0:T(8,128)S(1)}) custom-call(s32[128]{0:T(128)} %live_ref.1, f32[3,5632]{1,0:T(4,128)} %field_hbm.3, f32[45,128]{1,0:T(8,128)S(1)} %collective-permute-done.near_ref, f32[36,128]{1,0:T(8,128)S(1)} %collective-permute-done.1.one_ref, ...), custom_call_target="tpu_custom_call" | custom-call | tf_op jit(solution)/shard_map/main/pallas_call | solution.py:291
  26.4 0.1 collective-permute-start.4
  26.5 1.2 %collective-permute-done.4.swap_ref = f32[36,128]{1,0:T(8,128)S(1)} collective-permute-done((f32[36,128]{1,0:T(8,128)S(1)}, f32[36,128]{1,0:T(8,128)S(1)}, u32[]{:S(2)}, u32[]{:S(2)}) %collective-permute-start.4) | collective-permute-done | bytes 18464 | tf_op jit(solution)/shard_map/ppermute | solution.py:257
  27.7 5.5 %collective-permute-start.5 = (f32[36,128]{1,0:T(8,128)S(1)}, f32[36,128]{1,0:T(8,128)S(1)}, u32[]{:S(2)}, u32[]{:S(2)}) collective-permute-start(f32[36,128]{1,0:T(8,128)S(1)} %pad_maximum_fusion.1), channel_id=1, source_target_pairs={{0,1},{1,3},{2,0},{3,5},{4,2},{5,7},{6,4},{7,9},{8,6},{9,11},{10,8... | collective-permute-start | bytes 55304 | tf_op jit(solution)/shard_map/ppermute | solution.py:268
  33.2 0.1 collective-permute-start.6
  33.3 7.1 %collective-permute-done.6.two_ref = f32[27,128]{1,0:T(8,128)S(1)} collective-permute-done((f32[27,128]{1,0:T(8,128)S(1)}, f32[27,128]{1,0:T(8,128)S(1)}, u32[]{:S(2)}, u32[]{:S(2)}) %collective-permute-start.6) | collective-permute-done | bytes 13856 | tf_op jit(solution)/shard_map/ppermute | solution.py:268
  40.4 0.0 collective-permute-done.5.one_ref
  40.4 0.1 collective-permute-start.7
  40.5 1.2 %collective-permute-done.7.last_ref = f32[36,128]{1,0:T(8,128)S(1)} collective-permute-done((f32[36,128]{1,0:T(8,128)S(1)}, f32[36,128]{1,0:T(8,128)S(1)}, u32[]{:S(2)}, u32[]{:S(2)}) %collective-permute-start.7) | collective-permute-done | bytes 18464 | tf_op jit(solution)/shard_map/ppermute | solution.py:257
  41.7 0.0 copy-done
  41.7 1.4 %spread.1 = f32[3,5632]{1,0:T(4,128)} custom-call(f32[66,256]{1,0:T(8,128)S(1)} %get-tuple-element.13.own_ref, f32[36,128]{1,0:T(8,128)S(1)} %collective-permute-done.4.swap_ref, f32[36,128]{1,0:T(8,128)S(1)} %collective-permute-done.5.one_ref, f32[27,128]{1,0:T(8,128)S(1)} %collective-permute-done.6.two_ref, f32[36,128]{1,0:T(8,128)S(1)} %collective-permute-done.7.last_ref, ...), custom_call_target="tpu_custom_call" | custom-call | tf_op jit(solution)/shard_map/spread/pallas_call | solution.py:317
  (15 shorter events, 0.1 us)
Async XLA Ops:
  0.0 41.7 %copy-start = (s32[8,384]{1,0:T(8,128)S(1)}, s32[8,384]{1,0:T(8,128)}, u32[]{:S(2)}) copy-start(s32[8,384]{1,0:T(8,128)} %send_ref.1) | copy-start | bytes 36868
  1.4 1.6 %collective-permute-start = (f32[45,128]{1,0:T(8,128)S(1)}, f32[45,128]{1,0:T(8,128)S(1)}, u32[]{:S(2)}, u32[]{:S(2)}) collective-permute-start(f32[45,128]{1,0:T(8,128)S(1)} %get-tuple-element.11), channel_id=1, source_target_pairs={{0,1},{1,0},{2,3},{3,2},{4,5},{5,4},{6,7},{7,6},{8,9},{9,8},{10,11... | collective-permute-start | bytes 69128 | tf_op jit(solution)/shard_map/ppermute | solution.py:257
  3.1 9.0 %collective-permute-start.1 = (f32[36,128]{1,0:T(8,128)S(1)}, f32[36,128]{1,0:T(8,128)S(1)}, u32[]{:S(2)}, u32[]{:S(2)}) collective-permute-start(f32[36,128]{1,0:T(8,128)S(1)} %pad_maximum_fusion), channel_id=1, source_target_pairs={{0,2},{1,0},{2,4},{3,1},{4,6},{5,3},{6,8},{7,5},{8,10},{9,7},{10,1... | collective-permute-start | bytes 55304 | tf_op jit(solution)/shard_map/ppermute | solution.py:268
  7.6 4.5 %collective-permute-start.2 = (f32[27,128]{1,0:T(8,128)S(1)}, f32[27,128]{1,0:T(8,128)S(1)}, u32[]{:S(2)}, u32[]{:S(2)}) collective-permute-start(f32[27,128]{1,0:T(8,128)S(1)} %pad_maximum_fusion.3), channel_id=1, source_target_pairs={{0,4},{1,0},{2,6},{3,2},{4,8},{5,1},{6,10},{7,3},{8,12},{9,5},{10,... | collective-permute-start | bytes 41480 | tf_op jit(solution)/shard_map/ppermute | solution.py:268
  12.1 2.2 %collective-permute-start.3 = (f32[27,128]{1,0:T(8,128)S(1)}, f32[27,128]{1,0:T(8,128)S(1)}, u32[]{:S(2)}, u32[]{:S(2)}) collective-permute-start(f32[27,128]{1,0:T(8,128)S(1)} %pad_maximum_fusion.4), channel_id=1, source_target_pairs={{0,1},{1,0},{2,3},{3,2},{4,5},{5,4},{6,7},{7,6},{8,9},{9,8},{10,11... | collective-permute-start | bytes 41480 | tf_op jit(solution)/shard_map/ppermute | solution.py:257
  26.4 1.3 %collective-permute-start.4 = (f32[36,128]{1,0:T(8,128)S(1)}, f32[36,128]{1,0:T(8,128)S(1)}, u32[]{:S(2)}, u32[]{:S(2)}) collective-permute-start(f32[36,128]{1,0:T(8,128)S(1)} %get-tuple-element.14), channel_id=1, source_target_pairs={{0,1},{1,0},{2,3},{3,2},{4,5},{5,4},{6,7},{7,6},{8,9},{9,8},{10,11... | collective-permute-start | bytes 55304 | tf_op jit(solution)/shard_map/ppermute | solution.py:257
  27.7 12.7 %collective-permute-start.5 = (f32[36,128]{1,0:T(8,128)S(1)}, f32[36,128]{1,0:T(8,128)S(1)}, u32[]{:S(2)}, u32[]{:S(2)}) collective-permute-start(f32[36,128]{1,0:T(8,128)S(1)} %pad_maximum_fusion.1), channel_id=1, source_target_pairs={{0,1},{1,3},{2,0},{3,5},{4,2},{5,7},{6,4},{7,9},{8,6},{9,11},{10,8... | collective-permute-start | bytes 55304 | tf_op jit(solution)/shard_map/ppermute | solution.py:268
  33.2 7.2 %collective-permute-start.6 = (f32[27,128]{1,0:T(8,128)S(1)}, f32[27,128]{1,0:T(8,128)S(1)}, u32[]{:S(2)}, u32[]{:S(2)}) collective-permute-start(f32[27,128]{1,0:T(8,128)S(1)} %pad_maximum_fusion.5), channel_id=1, source_target_pairs={{0,1},{1,5},{2,3},{3,7},{4,0},{5,9},{6,2},{7,11},{8,4},{9,13},{10,... | collective-permute-start | bytes 41480 | tf_op jit(solution)/shard_map/ppermute | solution.py:268
  40.4 1.3 %collective-permute-start.7 = (f32[36,128]{1,0:T(8,128)S(1)}, f32[36,128]{1,0:T(8,128)S(1)}, u32[]{:S(2)}, u32[]{:S(2)}) collective-permute-start(f32[36,128]{1,0:T(8,128)S(1)} %pad_maximum_fusion.2), channel_id=1, source_target_pairs={{0,1},{1,0},{2,3},{3,2},{4,5},{5,4},{6,7},{7,6},{8,9},{9,8},{10,11... | collective-permute-start | bytes 55304 | tf_op jit(solution)/shard_map/ppermute | solution.py:257
where the time goes:
time: 43.8 us; the launch traced here: 43 us
  waiting for transfers between devices  15.2 us (35%)
  Pallas kernels  14.9 us (34%)
  starting transfers between devices  12.8 us (29%)
    pallas_call x1, Pallas kernels, body(): pl.pallas_call(main_kernel, out_shape=(f(3 * OWN_ROWS, WIDE), f(36, LANES...  12.1 us
    ppermute x4, waiting for transfers between devices, along(): return lax.ppermute(x, 'dom', list(route.items()))  11.1 us
    ppermute x4, starting transfers between devices, along(): return lax.ppermute(x, 'dom', list(route.items()))  10.5 us
    ppermute x4, waiting for transfers between devices, across(): lax.ppermute(x, 'dom', [(i, i ^ 1) for i in range(lax.axis_size('dom'))])  4.04 us
    ppermute x4, starting transfers between devices, across(): lax.ppermute(x, 'dom', [(i, i ^ 1) for i in range(lax.axis_size('dom'))])  2.32 us
    pallas_call x1, Pallas kernels, body(): pl.pallas_call(pick_kernel, out_shape=(f(45, LANES), f(27, LANES)), in_sp...  1.43 us
    pallas_call x1, Pallas kernels, body(): pl.pallas_call(spread_kernel, out_shape=f(3, NODES), in_specs=[VMEM] * 6,...  1.36 us
  transfers between devices with their start and end apart: 8, of which 6 were waited for; matrix products, arithmetic and copies ran while one was open for 0% of the time, Pallas kernels for 0%

commit v1 on v0

--- a/solution.py
+++ b/solution.py
@@ -4,6 +4,7 @@
 from jax.experimental import pallas as pl
 from jax.experimental.pallas import tpu as pltpu
 from jax.sharding import PartitionSpec as P
+
 
 F32 = jnp.float32
 BF16 = jnp.bfloat16
@@ -17,6 +18,7 @@
 SLOTS = NODES + 8 * GHOST
 OWN_ROWS = NODES // WIDE
 ALL_ROWS = SLOTS // WIDE
+GHOST_ROWS = ALL_ROWS - OWN_ROWS
 TILES = BLK // LANES
 VMEM = pl.BlockSpec(memory_space=pltpu.VMEM)
 HBM = pl.BlockSpec(memory_space=pltpu.HBM)
@@ -36,6 +38,43 @@
     for s in range(1, 6):
         u = jnp.where(q >= s * rows, q - s * rows, u)
     return jnp.where(q >= 6 * rows, -1, u).astype(F32)
+
+
+def table_rows(rows):
+    return pad16(6 * rows)
+
+
+def select_parts(rows):
+    per = 2 * rows
+    out, seen = [], {}
+    for g in range(-(-3 * per // 8)):
+        for c in sorted({min(8 * g // per, 2), min((8 * g + 7) // per, 2)}):
+            key = (max(8 * g, c * per) - c * per, min(8 * g + 8, c * per + per) - c * per, (c * per) % 8)
+            if key not in seen:
+                upper = row_upper(rows, 8 * g, 8)
+                q = iota_rows(8) + 8 * g
+                if 8 * g < c * per or 8 * g + 8 > c * per + per:
+                    upper = jnp.where((q >= c * per) & (q < c * per + per), upper, -1.0)
+                seen[key] = upper
+            out.append((g, c, key))
+    return out, seen
+
+
+def select_sums(parts, row, got, lanes):
+    order, uppers = parts
+    here = jnp.broadcast_to(row, (8, LANES))
+    hits, sums = {}, [jnp.zeros((8, LANES), F32)] * 3
+    for g, c, key in order:
+        if key not in hits:
+            hits[key] = uppers[key] == here
+        sums[c] = jnp.where(hits[key], got[8 * g:8 * g + 8, lanes:lanes + LANES], sums[c])
+    return sums
+
+
+def fill(tf, rows, x, c, h):
+    hi, low = split(x)
+    for part, y in ((0, hi), (1, low)):
+        tf[pl.ds((c * 2 + part) * rows + h // 2, 1), pl.ds((h % 2) * LANES, LANES)] = y
 
 
 def lower_parts():
@@ -83,12 +122,13 @@
     return jnp.where(side() == 1, pltpu.roll(x, 4, axis=0), x)
 
 
-def pick_kernel(field_hbm, send_hbm, swap_ref, out_ref, field_ref, send_ref, sem):
-    copies = [pltpu.make_async_copy(field_hbm, field_ref, sem.at[0]), pltpu.make_async_copy(send_hbm, send_ref, sem.at[1])]
+def pick_kernel(field_hbm, send_hbm, conn_hbm, swap_ref, out_ref, field_ref, conn_ref, send_ref, sem):
+    copies = [pltpu.make_async_copy(field_hbm, field_ref, sem.at[0]), pltpu.make_async_copy(send_hbm, send_ref, sem.at[1]),
+              pltpu.make_async_copy(conn_hbm, conn_ref, sem.at[2])]
     for copy in copies:
         copy.start()
-    for copy in copies:
-        copy.wait()
+    copies[0].wait()
+    copies[1].wait()
     place = {0: (swap_ref, 0), 4: (swap_ref, 9), 5: (swap_ref, 18), 6: (swap_ref, 27), 7: (swap_ref, 36),
              1: (out_ref, 0), 2: (out_ref, 9), 3: (out_ref, 18)}
     for j in range(3):
@@ -104,40 +144,61 @@
             for m in range(8):
                 ref, base = place[m]
                 ref[pl.ds(base + c * 3 + j, 1), :] = total[c][m:m + 1, :]
-
-
-def main_kernel(live_ref, field_hbm, near_ref, one_ref, two_ref, last_ref, conn_hbm, blocks_ref,
-                own_ref, swap_ref, one_out_ref, two_out_ref,
-                field_ref, conn_ref, early, stiff, sem, tf, lo, up, vals, high, low, total):
+    copies[2].wait()
+
+
+def prep_kernel(live_ref, field_ref, conn_ref, after_ref, blocks_hbm, stiff_ref, sums_ref, lo_ref, up_ref, sem, tf):
+    del after_ref
     n = live_ref[lax.axis_index("dom")]
-    second = side() == 1
-    field_copy = pltpu.make_async_copy(field_hbm, field_ref, early.at[0])
-    conn_copy = pltpu.make_async_copy(conn_hbm, conn_ref, early.at[1])
-    field_copy.start()
-    conn_copy.start()
 
     def fetch(b):
-        cols = pl.ds(pl.multiple_of(b * BLK, BLK), BLK)
-        return pltpu.make_async_copy(blocks_ref.at[:, :, cols], stiff.at[b], sem.at[b])
+        return pltpu.make_async_copy(blocks_hbm.at[:, :, pl.ds(pl.multiple_of(b * BLK, BLK), BLK)], stiff_ref.at[b], sem.at[b])
 
     def start(b, _):
         fetch(b).start()
         return 0
 
+    def wait(b, _):
+        fetch(b).wait()
+        return 0
+
     lax.fori_loop(0, n, start, 0)
-
-    tf[pl.ds(200, 8), :] = jnp.zeros((8, WIDE), F32)
-
-    def fill(x, c, h):
-        hi, low = split(x)
-        for part, y in ((0, hi), (1, low)):
-            tf[pl.ds((c * 2 + part) * ALL_ROWS + h // 2, 1), pl.ds((h % 2) * LANES, LANES)] = y
-
-    field_copy.wait()
+    used = 6 * OWN_ROWS
+    tf[pl.ds(used // 8 * 8, tf.shape[0] - used // 8 * 8), :] = jnp.zeros((tf.shape[0] - used // 8 * 8, WIDE), F32)
     for h in range(NODES // LANES):
         x = field_ref[:, pl.ds(h * LANES, LANES)]
         for c in range(3):
-            fill(x[c:c + 1, :], c, h)
+            fill(tf, OWN_ROWS, x[c:c + 1, :], c, h)
+    table = tf[...].astype(BF16)
+    lowers, parts = lower_parts(), select_parts(OWN_ROWS)
+
+    def step(b, _):
+        block = pl.ds(pl.multiple_of(b * BLK, BLK), BLK)
+        index = conn_ref[:, block]
+        lo_ref[b] = (index & (WIDE - 1)).astype(F32)
+        up_ref[b] = (index >> 8).astype(F32)
+        for a in range(10):
+            for t2 in range(TILES // 2):
+                cols = [pl.ds((2 * t2 + s) * LANES, LANES) for s in range(2)]
+                hot = jnp.concatenate([one_hot(lowers, lo_ref[b, pl.ds(a, 1), c]) for c in cols], axis=1)
+                got = jnp.dot(table, hot, preferred_element_type=F32)
+                for s in range(2):
+                    sums = select_sums(parts, up_ref[b, pl.ds(a, 1), cols[s]], got, s * LANES)
+                    for c in range(3):
+                        sums_ref[b, (a * TILES + 2 * t2 + s) * 3 + c] = sums[c]
+        return 0
+
+    lax.fori_loop(0, n, step, 0)
+    lax.fori_loop(0, n, wait, 0)
+
+
+def main_kernel(live_ref, near_ref, one_ref, two_ref, last_ref, stiff_ref, sums_ref, lo_ref, up_ref,
+                own_ref, swap_ref, one_out_ref, two_out_ref, tf, vals, high, low, total):
+    n = live_ref[lax.axis_index("dom")]
+    second = side() == 1
+
+    used = 6 * GHOST_ROWS
+    tf[pl.ds(used, tf.shape[0] - used), :] = jnp.zeros((tf.shape[0] - used, WIDE), F32)
     source = {0: (one_ref, 9), 1: (one_ref, 0), 2: (two_ref, 9), 3: (two_ref, 0),
               4: (near_ref, 0), 5: (last_ref, 9), 6: (last_ref, 0), 7: (last_ref, 18)}
     ghost = [source[m][0][pl.ds(source[m][1], 9), :] for m in range(8)]
@@ -146,57 +207,40 @@
         for c in range(3):
             for j in range(3):
                 q = c * 3 + j
-                fill(bundle[q:q + 1, :], c, NODES // LANES + 3 * k + j)
+                fill(tf, GHOST_ROWS, bundle[q:q + 1, :], c, 3 * k + j)
     table = tf[...].astype(BF16)
-    lowers, uppers = lower_parts(), upper_parts(ALL_ROWS)
-    per = 2 * ALL_ROWS
-    even = [row_upper(ALL_ROWS, 8 * g, 8) for g in range(9)]
-    odd = [row_upper(ALL_ROWS, 8 * g, 8) for g in range(8, 17)]
-    head = iota_rows(8) < per % 8
-    even[8] = jnp.where(head, even[8], -1.0)
-    odd[0] = jnp.where(head, -1.0, odd[0])
     total[...] = jnp.zeros_like(total)
-    conn_copy.wait()
+    lowers, uppers, parts = lower_parts(), upper_parts(ALL_ROWS), select_parts(GHOST_ROWS)
 
     def step(b, _):
-        index = conn_ref[:, pl.ds(pl.multiple_of(b * BLK, BLK), BLK)]
-        lo[...] = (index & (WIDE - 1)).astype(F32)
-        up[...] = (index >> 8).astype(F32)
+        hots = []
         for a in range(10):
             for t2 in range(TILES // 2):
                 cols = [pl.ds((2 * t2 + s) * LANES, LANES) for s in range(2)]
-                hot = jnp.concatenate([one_hot(lowers, lo[pl.ds(a, 1), c]) for c in cols], axis=1)
+                hot = jnp.concatenate([one_hot(lowers, lo_ref[b, pl.ds(a, 1), c]) for c in cols], axis=1)
+                hots.append(hot)
                 got = jnp.dot(table, hot, preferred_element_type=F32)
                 for s in range(2):
-                    here = jnp.broadcast_to(up[pl.ds(a, 1), cols[s]], (8, LANES))
-                    sums = [jnp.zeros((8, LANES), F32)] * 3
-                    for g in range(9):
-                        hit = even[g] == here
-                        for c in (0, 2):
-                            q = 8 * g + c * per
-                            sums[c] = jnp.where(hit, got[q:q + 8, s * LANES:(s + 1) * LANES], sums[c])
-                        q = 64 + 8 * g
-                        sums[1] = jnp.where(odd[g] == here, got[q:q + 8, s * LANES:(s + 1) * LANES], sums[1])
+                    sums = select_sums(parts, up_ref[b, pl.ds(a, 1), cols[s]] - OWN_ROWS, got, s * LANES)
                     for c in range(3):
+                        sums[c] = sums[c] + sums_ref[b, (a * TILES + 2 * t2 + s) * 3 + c]
                         vals[pl.ds(c * 10 + a, 1), cols[s]] = jnp.sum(sums[c], axis=0, keepdims=True)
-        fetch(b).wait()
         for t in range(TILES):
             cols = pl.ds(t * LANES, LANES)
             v = vals[:, cols]
             for i in range(30):
-                k = stiff[b, i, :, cols].astype(F32)
+                k = stiff_ref[b, i, :, cols].astype(F32)
                 high[pl.ds(i, 1), cols] = jnp.sum(k * v, axis=0, keepdims=True)
         high[...], low[...] = split(high[...])
         acc = None
         for a in range(10):
             for t2 in range(TILES // 2):
-                hot, put = [], []
+                put = []
                 for s in range(2):
                     cols = pl.ds((2 * t2 + s) * LANES, LANES)
-                    hot.append(one_hot(lowers, lo[pl.ds(a, 1), cols]))
                     values = [ref[pl.ds(c * 10 + a, 1), cols] for c in range(3) for ref in (high, low)]
-                    put.append(placed(uppers, up[pl.ds(a, 1), cols], values, ALL_ROWS))
-                part = lax.dot_general(jnp.concatenate(put, axis=1), jnp.concatenate(hot, axis=1), (((1,), (1,)), ((), ())),
+                    put.append(placed(uppers, up_ref[b, pl.ds(a, 1), cols], values, ALL_ROWS))
+                part = lax.dot_general(jnp.concatenate(put, axis=1), hots[a * (TILES // 2) + t2], (((1,), (1,)), ((), ())),
                                        preferred_element_type=F32)
                 acc = part if acc is None else acc + part
         total[...] += acc
@@ -278,38 +322,48 @@
 
 def body(field, blocks, connectivity, send_nodes, live_blocks):
     f = lambda *s: jax.ShapeDtypeStruct(s, F32)
-    swap, out = pl.pallas_call(
-        pick_kernel, out_shape=(f(45, LANES), f(27, LANES)), in_specs=[HBM] * 2, out_specs=(VMEM,) * 2,
-        scratch_shapes=[pltpu.VMEM((3, NODES), F32), pltpu.VMEM((8, GHOST), jnp.int32), pltpu.SemaphoreType.DMA((2,))],
-        compiler_params=params(1024), name="pick",
-    )(in_hbm(field), in_hbm(send_nodes))
+    swap, out, field_near, conn_near = pl.pallas_call(
+        pick_kernel,
+        out_shape=(f(45, LANES), f(27, LANES), pltpu.VMEM((3, NODES), F32), pltpu.VMEM((10, ELEMS), jnp.int32)),
+        in_specs=[HBM] * 3,
+        out_specs=(VMEM,) * 4,
+        scratch_shapes=[pltpu.VMEM((8, GHOST), jnp.int32), pltpu.SemaphoreType.DMA((3,))],
+        compiler_params=params(1024),
+        name="pick",
+    )(in_hbm(field), in_hbm(send_nodes), in_hbm(connectivity))
     near = across(swap)
     one = along(jnp.concatenate([out[:9], near[9:18], out[9:18], near[18:27]]), 1)
     two = along(jnp.concatenate([out[18:], near[27:]]), 2)
     last = across(jnp.concatenate([one[18:], two[18:]]))
-    rows = pad16(6 * ALL_ROWS)
+    smem = pl.BlockSpec(memory_space=pltpu.SMEM)
+    prep = pl.pallas_call(
+        prep_kernel,
+        out_shape=(pltpu.VMEM((NBLK, 30, 30, BLK), BF16), pltpu.VMEM((NBLK, 30 * TILES, 8, LANES), F32),
+                   pltpu.VMEM((NBLK, 10, BLK), F32), pltpu.VMEM((NBLK, 10, BLK), F32)),
+        in_specs=[smem, VMEM, VMEM, VMEM, HBM],
+        out_specs=(VMEM,) * 4,
+        scratch_shapes=[pltpu.SemaphoreType.DMA((NBLK,)), pltpu.VMEM((table_rows(OWN_ROWS), WIDE), F32)],
+        compiler_params=params(4096),
+        cost_estimate=pl.CostEstimate(flops=2 * 10**10, bytes_accessed=2**23, transcendentals=0),
+        name="prep",
+    )
+    stiff, sums, lo, up = prep(in_hbm(live_blocks), field_near, conn_near, near, in_hbm(blocks))
     own, swap, one_out, two_out = pl.pallas_call(
         main_kernel,
         out_shape=(f(3 * OWN_ROWS, WIDE), f(36, LANES), f(18, LANES), f(18, LANES)),
-        in_specs=[pl.BlockSpec(memory_space=pltpu.SMEM), HBM] + [VMEM] * 4 + [HBM] * 2,
+        in_specs=[smem] + [VMEM] * 8,
         out_specs=(VMEM,) * 4,
         scratch_shapes=[
-            pltpu.VMEM((3, NODES), F32),
-            pltpu.VMEM((10, ELEMS), jnp.int32),
-            pltpu.SemaphoreType.DMA((2,)),
-            pltpu.VMEM((NBLK, 30, 30, BLK), BF16),
-            pltpu.SemaphoreType.DMA((NBLK,)),
-            pltpu.VMEM((rows, WIDE), F32),
-            pltpu.VMEM((10, BLK), F32),
-            pltpu.VMEM((10, BLK), F32),
+            pltpu.VMEM((table_rows(GHOST_ROWS), WIDE), F32),
             pltpu.VMEM((30, BLK), F32),
             pltpu.VMEM((30, BLK), F32),
             pltpu.VMEM((30, BLK), F32),
-            pltpu.VMEM((rows, WIDE), F32),
+            pltpu.VMEM((table_rows(ALL_ROWS), WIDE), F32),
         ],
-        compiler_params=params(32768),
+        compiler_params=params(16384),
+        cost_estimate=pl.CostEstimate(flops=2 * 10**10, bytes_accessed=2**23, transcendentals=0),
         name="main",
-    )(in_hbm(live_blocks), in_hbm(field), near, one, two, last, in_hbm(connectivity), in_hbm(blocks))
+    )(in_hbm(live_blocks), near, one, two, last, stiff, sums, lo, up)
     swapped = across(swap)
     one_in = along(jnp.concatenate([one_out, swapped[:18]]), -1)
     two_in = along(jnp.concatenate([two_out, swapped[18:27]]), -2)

time: 43.8 us -> 44.1 us (level)
  the two profiles are of different devices: /device:TPU:65 before, /device:TPU:33 now
where the time goes in v1:
time: 44.1 us; the launch traced here: 43.4 us
  Pallas kernels  16 us (36%)
  waiting for transfers between devices  14.3 us (32%)
  starting transfers between devices  13 us (29%)
    ppermute x4, waiting for transfers between devices, along(): return lax.ppermute(x, 'dom', list(route.items()))  11.1 us
    ppermute x4, starting transfers between devices, along(): return lax.ppermute(x, 'dom', list(route.items()))  10.6 us
    pallas_call x1, Pallas kernels, body(): pl.pallas_call(main_kernel, out_shape=(f(3 * OWN_ROWS, WIDE), f(36, LANES...  9.4 us
    pallas_call x1, Pallas kernels, body(): prep(in_hbm(live_blocks), field_near, conn_near, near, in_hbm(blocks))  3.76 us
    ppermute x4, waiting for transfers between devices, across(): lax.ppermute(x, 'dom', [(i, i ^ 1) for i in range(lax.axis_size('dom'))])  3.2 us
    ppermute x4, starting transfers between devices, across(): lax.ppermute(x, 'dom', [(i, i ^ 1) for i in range(lax.axis_size('dom'))])  2.32 us
    pallas_call x1, Pallas kernels, body(): pl.pallas_call(pick_kernel, out_shape=(f(45, LANES), f(27, LANES), pltpu....  1.43 us
    pallas_call x1, Pallas kernels, body(): pl.pallas_call(spread_kernel, out_shape=f(3, NODES), in_specs=[VMEM] * 6,...  1.36 us
  transfers between devices with their start and end apart: 8, of which 5 were waited for; matrix products, arithmetic and copies ran while one was open for 0% of the time, Pallas kernels for 9%

profile of v1, /device:TPU:33, one launch (start us, length us, event | category | flops | bytes accessed | tf_op | source)
XLA Modules:
  0.0 43.4 jit_solution(18239853596480457147)
XLA Ops:
  0.0 1.4 %pick.1 = (f32[45,128]{1,0:T(8,128)S(1)}, f32[27,128]{1,0:T(8,128)S(1)}, f32[3,5632]{1,0:T(4,128)S(1)}, s32[10,4096]{1,0:T(8,128)S(1)}) custom-call(f32[3,5632]{1,0:T(4,128)} %field_hbm.1, s32[8,384]{1,0:T(8,128)} %send_ref.1, s32[10,4096]{1,0:T(8,128)} %conn_hbm.1), custom_call_target="tpu_custom_call" | custom-call | tf_op jit(solution)/shard_map/pick/pallas_call | solution.py:325
  1.4 0.8 %collective-permute-start = (f32[45,128]{1,0:T(8,128)S(1)}, f32[45,128]{1,0:T(8,128)S(1)}, u32[]{:S(2)}, u32[]{:S(2)}) collective-permute-start(f32[45,128]{1,0:T(8,128)S(1)} %get-tuple-element.17), channel_id=1, source_target_pairs={{0,1},{1,0},{2,3},{3,2},{4,5},{5,4},{6,7},{7,6},{8,9},{9,8},{10,11... | collective-permute-start | bytes 69128 | tf_op jit(solution)/shard_map/ppermute | solution.py:301
  2.2 0.8 %collective-permute-done.after_ref.near_ref = f32[45,128]{1,0:T(8,128)S(1)} collective-permute-done((f32[45,128]{1,0:T(8,128)S(1)}, f32[45,128]{1,0:T(8,128)S(1)}, u32[]{:S(2)}, u32[]{:S(2)}) %collective-permute-start) | collective-permute-done | bytes 23072 | tf_op jit(solution)/shard_map/ppermute | solution.py:301
  3.1 4.5 %collective-permute-start.1 = (f32[36,128]{1,0:T(8,128)S(1)}, f32[36,128]{1,0:T(8,128)S(1)}, u32[]{:S(2)}, u32[]{:S(2)}) collective-permute-start(f32[36,128]{1,0:T(8,128)S(1)} %pad_maximum_fusion), channel_id=1, source_target_pairs={{0,2},{1,0},{2,4},{3,1},{4,6},{5,3},{6,8},{7,5},{8,10},{9,7},{10,1... | collective-permute-start | bytes 55304 | tf_op jit(solution)/shard_map/ppermute | solution.py:312
  7.6 0.4 collective-permute-start.2
  8.0 4.0 %collective-permute-done.2.two_ref = f32[27,128]{1,0:T(8,128)S(1)} collective-permute-done((f32[27,128]{1,0:T(8,128)S(1)}, f32[27,128]{1,0:T(8,128)S(1)}, u32[]{:S(2)}, u32[]{:S(2)}) %collective-permute-start.2) | collective-permute-done | bytes 13856 | tf_op jit(solution)/shard_map/ppermute | solution.py:312
  12.1 0.0 collective-permute-done.1.one_ref
  12.1 1.4 %collective-permute-start.3 = (f32[27,128]{1,0:T(8,128)S(1)}, f32[27,128]{1,0:T(8,128)S(1)}, u32[]{:S(2)}, u32[]{:S(2)}) collective-permute-start(f32[27,128]{1,0:T(8,128)S(1)} %pad_maximum_fusion.4), channel_id=1, source_target_pairs={{0,1},{1,0},{2,3},{3,2},{4,5},{5,4},{6,7},{7,6},{8,9},{9,8},{10,11... | collective-permute-start | bytes 41480 | tf_op jit(solution)/shard_map/ppermute | solution.py:301
  13.5 3.8 %prep.1 = (bf16[8,30,30,512]{3,2,1,0:T(8,128)(2,1)S(1)}, f32[8,120,8,128]{3,2,1,0:T(8,128)S(1)}, f32[8,10,512]{2,1,0:T(8,128)S(1)}, f32[8,10,512]{2,1,0:T(8,128)S(1)}) custom-call(s32[128]{0:T(128)} %live_ref.3, f32[3,5632]{1,0:T(4,128)S(1)} %get-tuple-element.19.field_ref, s32[10,4096]{1,0:T(8,128)S(1)} %get-tuple-element.20.conn_ref, ...), custom_call_target="tpu_custom_call" | custom-call | flops 20000000000 | bytes 8388608 | tf_op jit(solution)/shard_map/prep/pallas_call | solution.py:350
  17.3 0.0 collective-permute-done.3.last_ref
  17.3 0.0 copy-start
  17.3 9.4 %main.1 = (f32[66,256]{1,0:T(8,128)S(1)}, f32[36,128]{1,0:T(8,128)S(1)}, f32[18,128]{1,0:T(8,128)S(1)}, f32[18,128]{1,0:T(8,128)S(1)}) custom-call(s32[128]{0:T(128)} %live_ref.3, f32[45,128]{1,0:T(8,128)S(1)} %collective-permute-done.after_ref.near_ref, f32[36,128]{1,0:T(8,128)S(1)} %collective-permute-done.1.one_ref, ...), custom_call_target="tpu_custom_call" | custom-call | flops 20000000000 | bytes 8388608 | tf_op jit(solution)/shard_map/main/pallas_call | solution.py:351
  26.7 0.1 collective-permute-start.4
  26.8 1.2 %collective-permute-done.4.swap_ref = f32[36,128]{1,0:T(8,128)S(1)} collective-permute-done((f32[36,128]{1,0:T(8,128)S(1)}, f32[36,128]{1,0:T(8,128)S(1)}, u32[]{:S(2)}, u32[]{:S(2)}) %collective-permute-start.4) | collective-permute-done | bytes 18464 | tf_op jit(solution)/shard_map/ppermute | solution.py:301
  28.0 5.6 %collective-permute-start.5 = (f32[36,128]{1,0:T(8,128)S(1)}, f32[36,128]{1,0:T(8,128)S(1)}, u32[]{:S(2)}, u32[]{:S(2)}) collective-permute-start(f32[36,128]{1,0:T(8,128)S(1)} %pad_maximum_fusion.1), channel_id=1, source_target_pairs={{0,1},{1,3},{2,0},{3,5},{4,2},{5,7},{6,4},{7,9},{8,6},{9,11},{10,8... | collective-permute-start | bytes 55304 | tf_op jit(solution)/shard_map/ppermute | solution.py:312
  33.6 0.1 collective-permute-start.6
  33.7 7.1 %collective-permute-done.6.two_ref = f32[27,128]{1,0:T(8,128)S(1)} collective-permute-done((f32[27,128]{1,0:T(8,128)S(1)}, f32[27,128]{1,0:T(8,128)S(1)}, u32[]{:S(2)}, u32[]{:S(2)}) %collective-permute-start.6) | collective-permute-done | bytes 13856 | tf_op jit(solution)/shard_map/ppermute | solution.py:312
  40.8 0.0 collective-permute-done.5.one_ref
  40.8 0.1 collective-permute-start.7
  40.9 1.2 %collective-permute-done.7.last_ref = f32[36,128]{1,0:T(8,128)S(1)} collective-permute-done((f32[36,128]{1,0:T(8,128)S(1)}, f32[36,128]{1,0:T(8,128)S(1)}, u32[]{:S(2)}, u32[]{:S(2)}) %collective-permute-start.7) | collective-permute-done | bytes 18464 | tf_op jit(solution)/shard_map/ppermute | solution.py:301
  42.1 0.0 copy-done
  42.1 1.4 %spread.1 = f32[3,5632]{1,0:T(4,128)} custom-call(f32[66,256]{1,0:T(8,128)S(1)} %get-tuple-element.25.own_ref, f32[36,128]{1,0:T(8,128)S(1)} %collective-permute-done.4.swap_ref, f32[36,128]{1,0:T(8,128)S(1)} %collective-permute-done.5.one_ref, f32[27,128]{1,0:T(8,128)S(1)} %collective-permute-done.6.two_ref, f32[36,128]{1,0:T(8,128)S(1)} %collective-permute-done.7.last_ref, ...), custom_call_target="tpu_custom_call" | custom-call | tf_op jit(solution)/shard_map/spread/pallas_call | solution.py:371
  (15 shorter events, 0.1 us)
Async XLA Ops:
  1.4 1.6 %collective-permute-start = (f32[45,128]{1,0:T(8,128)S(1)}, f32[45,128]{1,0:T(8,128)S(1)}, u32[]{:S(2)}, u32[]{:S(2)}) collective-permute-start(f32[45,128]{1,0:T(8,128)S(1)} %get-tuple-element.17), channel_id=1, source_target_pairs={{0,1},{1,0},{2,3},{3,2},{4,5},{5,4},{6,7},{7,6},{8,9},{9,8},{10,11... | collective-permute-start | bytes 69128 | tf_op jit(solution)/shard_map/ppermute | solution.py:301
  3.1 9.0 %collective-permute-start.1 = (f32[36,128]{1,0:T(8,128)S(1)}, f32[36,128]{1,0:T(8,128)S(1)}, u32[]{:S(2)}, u32[]{:S(2)}) collective-permute-start(f32[36,128]{1,0:T(8,128)S(1)} %pad_maximum_fusion), channel_id=1, source_target_pairs={{0,2},{1,0},{2,4},{3,1},{4,6},{5,3},{6,8},{7,5},{8,10},{9,7},{10,1... | collective-permute-start | bytes 55304 | tf_op jit(solution)/shard_map/ppermute | solution.py:312
  7.6 4.5 %collective-permute-start.2 = (f32[27,128]{1,0:T(8,128)S(1)}, f32[27,128]{1,0:T(8,128)S(1)}, u32[]{:S(2)}, u32[]{:S(2)}) collective-permute-start(f32[27,128]{1,0:T(8,128)S(1)} %pad_maximum_fusion.3), channel_id=1, source_target_pairs={{0,4},{1,0},{2,6},{3,2},{4,8},{5,1},{6,10},{7,3},{8,12},{9,5},{10,... | collective-permute-start | bytes 41480 | tf_op jit(solution)/shard_map/ppermute | solution.py:312
  12.1 5.2 %collective-permute-start.3 = (f32[27,128]{1,0:T(8,128)S(1)}, f32[27,128]{1,0:T(8,128)S(1)}, u32[]{:S(2)}, u32[]{:S(2)}) collective-permute-start(f32[27,128]{1,0:T(8,128)S(1)} %pad_maximum_fusion.4), channel_id=1, source_target_pairs={{0,1},{1,0},{2,3},{3,2},{4,5},{5,4},{6,7},{7,6},{8,9},{9,8},{10,11... | collective-permute-start | bytes 41480 | tf_op jit(solution)/shard_map/ppermute | solution.py:301
  17.3 24.8 %copy-start = (s32[8,384]{1,0:T(8,128)S(1)}, s32[8,384]{1,0:T(8,128)}, u32[]{:S(2)}) copy-start(s32[8,384]{1,0:T(8,128)} %send_ref.1) | copy-start | bytes 36868
  26.7 1.3 %collective-permute-start.4 = (f32[36,128]{1,0:T(8,128)S(1)}, f32[36,128]{1,0:T(8,128)S(1)}, u32[]{:S(2)}, u32[]{:S(2)}) collective-permute-start(f32[36,128]{1,0:T(8,128)S(1)} %get-tuple-element.26), channel_id=1, source_target_pairs={{0,1},{1,0},{2,3},{3,2},{4,5},{5,4},{6,7},{7,6},{8,9},{9,8},{10,11... | collective-permute-start | bytes 55304 | tf_op jit(solution)/shard_map/ppermute | solution.py:301
  28.0 12.8 %collective-permute-start.5 = (f32[36,128]{1,0:T(8,128)S(1)}, f32[36,128]{1,0:T(8,128)S(1)}, u32[]{:S(2)}, u32[]{:S(2)}) collective-permute-start(f32[36,128]{1,0:T(8,128)S(1)} %pad_maximum_fusion.1), channel_id=1, source_target_pairs={{0,1},{1,3},{2,0},{3,5},{4,2},{5,7},{6,4},{7,9},{8,6},{9,11},{10,8... | collective-permute-start | bytes 55304 | tf_op jit(solution)/shard_map/ppermute | solution.py:312
  33.6 7.2 %collective-permute-start.6 = (f32[27,128]{1,0:T(8,128)S(1)}, f32[27,128]{1,0:T(8,128)S(1)}, u32[]{:S(2)}, u32[]{:S(2)}) collective-permute-start(f32[27,128]{1,0:T(8,128)S(1)} %pad_maximum_fusion.5), channel_id=1, source_target_pairs={{0,1},{1,5},{2,3},{3,7},{4,0},{5,9},{6,2},{7,11},{8,4},{9,13},{10,... | collective-permute-start | bytes 41480 | tf_op jit(solution)/shard_map/ppermute | solution.py:312
  40.8 1.3 %collective-permute-start.7 = (f32[36,128]{1,0:T(8,128)S(1)}, f32[36,128]{1,0:T(8,128)S(1)}, u32[]{:S(2)}, u32[]{:S(2)}) collective-permute-start(f32[36,128]{1,0:T(8,128)S(1)} %pad_maximum_fusion.2), channel_id=1, source_target_pairs={{0,1},{1,0},{2,3},{3,2},{4,5},{5,4},{6,7},{7,6},{8,9},{9,8},{10,11... | collective-permute-start | bytes 55304 | tf_op jit(solution)/shard_map/ppermute | solution.py:301

commit v2 on v1

--- a/solution.py
+++ b/solution.py
@@ -20,6 +20,7 @@
 ALL_ROWS = SLOTS // WIDE
 GHOST_ROWS = ALL_ROWS - OWN_ROWS
 TILES = BLK // LANES
+UNROLL = 2
 VMEM = pl.BlockSpec(memory_space=pltpu.VMEM)
 HBM = pl.BlockSpec(memory_space=pltpu.HBM)
 
@@ -118,13 +119,18 @@
     return lax.rem(lax.axis_index("dom"), 2)
 
 
+def own_live(live_ref):
+    here = lax.broadcasted_iota(jnp.int32, (1, LANES), 1) == lax.axis_index("dom")
+    return jnp.sum(jnp.where(here, live_ref[...].astype(F32), 0.0)).astype(jnp.int32)
+
+
 def by_label(x):
     return jnp.where(side() == 1, pltpu.roll(x, 4, axis=0), x)
 
 
-def pick_kernel(field_hbm, send_hbm, conn_hbm, swap_ref, out_ref, field_ref, conn_ref, send_ref, sem):
+def pick_kernel(field_hbm, send_hbm, conn_hbm, live_hbm, swap_ref, out_ref, field_ref, conn_ref, live_ref, send_ref, sem):
     copies = [pltpu.make_async_copy(field_hbm, field_ref, sem.at[0]), pltpu.make_async_copy(send_hbm, send_ref, sem.at[1]),
-              pltpu.make_async_copy(conn_hbm, conn_ref, sem.at[2])]
+              pltpu.make_async_copy(conn_hbm, conn_ref, sem.at[2]), pltpu.make_async_copy(live_hbm, live_ref, sem.at[3])]
     for copy in copies:
         copy.start()
     copies[0].wait()
@@ -145,11 +151,12 @@
                 ref, base = place[m]
                 ref[pl.ds(base + c * 3 + j, 1), :] = total[c][m:m + 1, :]
     copies[2].wait()
+    copies[3].wait()
 
 
 def prep_kernel(live_ref, field_ref, conn_ref, after_ref, blocks_hbm, stiff_ref, sums_ref, lo_ref, up_ref, sem, tf):
     del after_ref
-    n = live_ref[lax.axis_index("dom")]
+    n = own_live(live_ref)
 
     def fetch(b):
         return pltpu.make_async_copy(blocks_hbm.at[:, :, pl.ds(pl.multiple_of(b * BLK, BLK), BLK)], stiff_ref.at[b], sem.at[b])
@@ -194,7 +201,7 @@
 
 def main_kernel(live_ref, near_ref, one_ref, two_ref, last_ref, stiff_ref, sums_ref, lo_ref, up_ref,
                 own_ref, swap_ref, one_out_ref, two_out_ref, tf, vals, high, low, total):
-    n = live_ref[lax.axis_index("dom")]
+    n = own_live(live_ref)
     second = side() == 1
 
     used = 6 * GHOST_ROWS
@@ -212,41 +219,73 @@
     total[...] = jnp.zeros_like(total)
     lowers, uppers, parts = lower_parts(), upper_parts(ALL_ROWS), select_parts(GHOST_ROWS)
 
-    def step(b, _):
-        hots = []
-        for a in range(10):
-            for t2 in range(TILES // 2):
-                cols = [pl.ds((2 * t2 + s) * LANES, LANES) for s in range(2)]
-                hot = jnp.concatenate([one_hot(lowers, lo_ref[b, pl.ds(a, 1), c]) for c in cols], axis=1)
-                hots.append(hot)
-                got = jnp.dot(table, hot, preferred_element_type=F32)
-                for s in range(2):
-                    sums = select_sums(parts, up_ref[b, pl.ds(a, 1), cols[s]] - OWN_ROWS, got, s * LANES)
-                    for c in range(3):
-                        sums[c] = sums[c] + sums_ref[b, (a * TILES + 2 * t2 + s) * 3 + c]
-                        vals[pl.ds(c * 10 + a, 1), cols[s]] = jnp.sum(sums[c], axis=0, keepdims=True)
-        for t in range(TILES):
-            cols = pl.ds(t * LANES, LANES)
-            v = vals[:, cols]
-            for i in range(30):
-                k = stiff_ref[b, i, :, cols].astype(F32)
-                high[pl.ds(i, 1), cols] = jnp.sum(k * v, axis=0, keepdims=True)
-        high[...], low[...] = split(high[...])
-        acc = None
-        for a in range(10):
-            for t2 in range(TILES // 2):
-                put = []
-                for s in range(2):
-                    cols = pl.ds((2 * t2 + s) * LANES, LANES)
-                    values = [ref[pl.ds(c * 10 + a, 1), cols] for c in range(3) for ref in (high, low)]
-                    put.append(placed(uppers, up_ref[b, pl.ds(a, 1), cols], values, ALL_ROWS))
-                part = lax.dot_general(jnp.concatenate(put, axis=1), hots[a * (TILES // 2) + t2], (((1,), (1,)), ((), ())),
-                                       preferred_element_type=F32)
-                acc = part if acc is None else acc + part
-        total[...] += acc
+    def gather(b, half, hots, vals):
+        def chunk(a):
+            cols = [pl.ds((2 * half + s) * LANES, LANES) for s in range(2)]
+            hots[a] = hot = jnp.concatenate([one_hot(lowers, lo_ref[b, pl.ds(a, 1), c]) for c in cols], axis=1).astype(jnp.float8_e4m3fn)
+            got = jnp.dot(table, hot, preferred_element_type=F32)
+            for s in range(2):
+                sums = select_sums(parts, up_ref[b, pl.ds(a, 1), cols[s]] - OWN_ROWS, got, s * LANES)
+                for c in range(3):
+                    both = sums[c] + sums_ref[b, (a * TILES + 2 * half + s) * 3 + c]
+                    vals[pl.ds(c * 10 + a, 1), pl.ds(s * LANES, LANES)] = jnp.sum(both, axis=0, keepdims=True)
+
+        return [lambda a=a: chunk(a) for a in range(10)]
+
+    def apply(b, half, vals, high, low):
+        def row(i):
+            for s in range(2):
+                cols = pl.ds(s * LANES, LANES)
+                k = stiff_ref[b, i, :, pl.ds((2 * half + s) * LANES, LANES)].astype(F32)
+                high[pl.ds(i, 1), cols] = jnp.sum(k * vals[:, cols], axis=0, keepdims=True)
+
+        def finish():
+            force = jnp.where(b < n, high[...], 0.0)
+            high[...], low[...] = split(force)
+
+        return [lambda i=i: row(i) for i in range(30)] + [finish]
+
+    def scatter(b, half, hots, high, low, acc):
+        def chunk(a):
+            put = []
+            for s in range(2):
+                cols = pl.ds(s * LANES, LANES)
+                values = [ref[pl.ds(c * 10 + a, 1), cols] for c in range(3) for ref in (high, low)]
+                row = up_ref[b, pl.ds(a, 1), pl.ds((2 * half + s) * LANES, LANES)]
+                put.append(placed(uppers, row, values, ALL_ROWS))
+            hot = hots[a]
+            part = lax.dot_general(jnp.concatenate(put, axis=1), hot, (((1,), (1,)), ((), ())), preferred_element_type=F32)
+            acc[0] = part if acc[0] is None else acc[0] + part
+
+        return [lambda a=a: chunk(a) for a in range(10)]
+
+    def together(*streams):
+        pieces = [((i + 1) / len(stream), k, i) for k, stream in enumerate(streams) for i in range(len(stream))]
+        for _, k, i in sorted(pieces):
+            streams[k][i]()
+
+    def step(trip, _):
+        units = [(UNROLL * trip + k, half) for k in range(UNROLL) for half in range(2)]
+        hots = [[None] * 10 for _ in units]
+        acc = [None]
+        buffers = [(vals.at[k], high.at[k], low.at[k]) for k in range(len(units))]
+        order = [("gather", k) for k in range(len(units))] + [("apply", 0)]
+        for k in range(len(units)):
+            order += ([("apply", k + 1)] if k + 1 < len(units) else []) + [("scatter", k)]
+        for kind, k in order:
+            streams = []
+            v, h, w = buffers[k]
+            if kind == "scatter":
+                streams.append(scatter(*units[k], hots[k], h, w, acc))
+            elif kind == "apply":
+                streams.append(apply(*units[k], v, h, w))
+            else:
+                streams.append(gather(*units[k], hots[k], v))
+            together(*streams)
+        total[...] += acc[0]
         return 0
 
-    lax.fori_loop(0, n, step, 0)
+    lax.fori_loop(0, lax.div(n + (UNROLL - 1), UNROLL), step, 0)
 
     for c in range(3):
         base = 2 * c * ALL_ROWS
@@ -320,57 +359,67 @@
     return pltpu.CompilerParams(vmem_limit_bytes=kib * 1024)
 
 
-def body(field, blocks, connectivity, send_nodes, live_blocks):
-    f = lambda *s: jax.ShapeDtypeStruct(s, F32)
-    swap, out, field_near, conn_near = pl.pallas_call(
-        pick_kernel,
-        out_shape=(f(45, LANES), f(27, LANES), pltpu.VMEM((3, NODES), F32), pltpu.VMEM((10, ELEMS), jnp.int32)),
-        in_specs=[HBM] * 3,
-        out_specs=(VMEM,) * 4,
-        scratch_shapes=[pltpu.VMEM((8, GHOST), jnp.int32), pltpu.SemaphoreType.DMA((3,))],
-        compiler_params=params(1024),
-        name="pick",
-    )(in_hbm(field), in_hbm(send_nodes), in_hbm(connectivity))
-    near = across(swap)
-    one = along(jnp.concatenate([out[:9], near[9:18], out[9:18], near[18:27]]), 1)
-    two = along(jnp.concatenate([out[18:], near[27:]]), 2)
-    last = across(jnp.concatenate([one[18:], two[18:]]))
-    smem = pl.BlockSpec(memory_space=pltpu.SMEM)
-    prep = pl.pallas_call(
+def rows_f32(*shape):
+    return jax.ShapeDtypeStruct(shape, F32)
+
+
+def prep_call():
+    return pl.pallas_call(
         prep_kernel,
         out_shape=(pltpu.VMEM((NBLK, 30, 30, BLK), BF16), pltpu.VMEM((NBLK, 30 * TILES, 8, LANES), F32),
                    pltpu.VMEM((NBLK, 10, BLK), F32), pltpu.VMEM((NBLK, 10, BLK), F32)),
-        in_specs=[smem, VMEM, VMEM, VMEM, HBM],
+        in_specs=[VMEM] * 4 + [HBM],
         out_specs=(VMEM,) * 4,
         scratch_shapes=[pltpu.SemaphoreType.DMA((NBLK,)), pltpu.VMEM((table_rows(OWN_ROWS), WIDE), F32)],
         compiler_params=params(4096),
         cost_estimate=pl.CostEstimate(flops=2 * 10**10, bytes_accessed=2**23, transcendentals=0),
         name="prep",
     )
-    stiff, sums, lo, up = prep(in_hbm(live_blocks), field_near, conn_near, near, in_hbm(blocks))
-    own, swap, one_out, two_out = pl.pallas_call(
+
+
+def main_call():
+    return pl.pallas_call(
         main_kernel,
-        out_shape=(f(3 * OWN_ROWS, WIDE), f(36, LANES), f(18, LANES), f(18, LANES)),
-        in_specs=[smem] + [VMEM] * 8,
+        out_shape=(rows_f32(3 * OWN_ROWS, WIDE), rows_f32(36, LANES), rows_f32(18, LANES), rows_f32(18, LANES)),
+        in_specs=[VMEM] * 9,
         out_specs=(VMEM,) * 4,
         scratch_shapes=[
             pltpu.VMEM((table_rows(GHOST_ROWS), WIDE), F32),
-            pltpu.VMEM((30, BLK), F32),
-            pltpu.VMEM((30, BLK), F32),
-            pltpu.VMEM((30, BLK), F32),
+            pltpu.VMEM((2 * UNROLL, 30, BLK // 2), F32),
+            pltpu.VMEM((2 * UNROLL, 30, BLK // 2), F32),
+            pltpu.VMEM((2 * UNROLL, 30, BLK // 2), F32),
             pltpu.VMEM((table_rows(ALL_ROWS), WIDE), F32),
         ],
         compiler_params=params(16384),
         cost_estimate=pl.CostEstimate(flops=2 * 10**10, bytes_accessed=2**23, transcendentals=0),
         name="main",
-    )(in_hbm(live_blocks), near, one, two, last, stiff, sums, lo, up)
+    )
+
+
+def body(field, blocks, connectivity, send_nodes, live_blocks):
+    swap, out, field_near, conn_near, live = pl.pallas_call(
+        pick_kernel,
+        out_shape=(rows_f32(45, LANES), rows_f32(27, LANES), pltpu.VMEM((3, NODES), F32), pltpu.VMEM((10, ELEMS), jnp.int32),
+                   pltpu.VMEM((1, LANES), jnp.int32)),
+        in_specs=[HBM] * 4,
+        out_specs=(VMEM,) * 5,
+        scratch_shapes=[pltpu.VMEM((8, GHOST), jnp.int32), pltpu.SemaphoreType.DMA((4,))],
+        compiler_params=params(1024),
+        name="pick",
+    )(in_hbm(field), in_hbm(send_nodes), in_hbm(connectivity), in_hbm(live_blocks.reshape(1, LANES)))
+    near = across(swap)
+    one = along(jnp.concatenate([out[:9], near[9:18], out[9:18], near[18:27]]), 1)
+    two = along(jnp.concatenate([out[18:], near[27:]]), 2)
+    last = across(jnp.concatenate([one[18:], two[18:]]))
+    stiff, sums, lo, up = prep_call()(live, field_near, conn_near, near, in_hbm(blocks))
+    own, swap, one_out, two_out = main_call()(live, near, one, two, last, stiff, sums, lo, up)
     swapped = across(swap)
     one_in = along(jnp.concatenate([one_out, swapped[:18]]), -1)
     two_in = along(jnp.concatenate([two_out, swapped[18:27]]), -2)
     back = across(jnp.concatenate([one_in[9:18], one_in[27:], two_in[9:]]))
     return pl.pallas_call(
         spread_kernel,
-        out_shape=f(3, NODES),
+        out_shape=rows_f32(3, NODES),
         in_specs=[VMEM] * 6,
         out_specs=VMEM,
         scratch_shapes=[

time: 44.1 us -> 42.9 us (0.973)
  Pallas kernels: 16 us -> 15.4 us
    pallas_call x4, Pallas kernels: 16 us -> 15.4 us  [the longest x1 9.33 us: body(): main_call()(live, near, one, two, last, stiff, sums, lo, up)]
  transfers between devices with their start and end apart: 8 -> 8, of which waited for: 5 -> 5; matrix products, arithmetic and copies ran while one was open for 0% -> 0% of each run, Pallas kernels for 9% -> 8%
where the time goes in v2:
time: 42.9 us; the launch traced here: 42.5 us
  Pallas kernels  15.4 us (36%)
  waiting for transfers between devices  14.3 us (33%)
  starting transfers between devices  12.6 us (29%)
    ppermute x4, waiting for transfers between devices, along(): return lax.ppermute(x, 'dom', list(route.items()))  11.1 us
    ppermute x4, starting transfers between devices, along(): return lax.ppermute(x, 'dom', list(route.items()))  10.3 us
    pallas_call x1, Pallas kernels, body(): main_call()(live, near, one, two, last, stiff, sums, lo, up)  9.33 us
    pallas_call x1, Pallas kernels, body(): prep_call()(live, field_near, conn_near, near, in_hbm(blocks))  3.22 us
    ppermute x4, waiting for transfers between devices, across(): lax.ppermute(x, 'dom', [(i, i ^ 1) for i in range(lax.axis_size('dom'))])  3.2 us
    ppermute x4, starting transfers between devices, across(): lax.ppermute(x, 'dom', [(i, i ^ 1) for i in range(lax.axis_size('dom'))])  2.32 us
    pallas_call x1, Pallas kernels, body(): pl.pallas_call(pick_kernel, out_shape=(rows_f32(45, LANES), rows_f32(27,...  1.44 us
    pallas_call x1, Pallas kernels, body(): pl.pallas_call(spread_kernel, out_shape=rows_f32(3, NODES), in_specs=[VME...  1.36 us
  transfers between devices with their start and end apart: 8, of which 5 were waited for; matrix products, arithmetic and copies ran while one was open for 0% of the time, Pallas kernels for 8%

profile of v2, /device:TPU:33, one launch (start us, length us, event | category | flops | bytes accessed | tf_op | source)
XLA Modules:
  0.0 42.5 jit_solution(2533308100025828768)
XLA Ops:
  0.0 1.4 %pick.1 = (f32[45,128]{1,0:T(8,128)S(1)}, f32[27,128]{1,0:T(8,128)S(1)}, f32[3,5632]{1,0:T(4,128)S(1)}, s32[10,4096]{1,0:T(8,128)S(1)}, s32[1,128]{1,0:T(1,128)S(1)}) custom-call(f32[3,5632]{1,0:T(4,128)} %field_hbm.1, s32[8,384]{1,0:T(8,128)} %send_ref.1, s32[10,4096]{1,0:T(8,128)} %conn_hbm.1, s32[1,128]{1,0:T(1,128)} %bitcast.1), custom_call_target="tpu_custom_call" | custom-call | tf_op jit(solution)/shard_map/pick/pallas_call | solution.py:400
  1.5 0.8 %collective-permute-start = (f32[45,128]{1,0:T(8,128)S(1)}, f32[45,128]{1,0:T(8,128)S(1)}, u32[]{:S(2)}, u32[]{:S(2)}) collective-permute-start(f32[45,128]{1,0:T(8,128)S(1)} %get-tuple-element.19), channel_id=1, source_target_pairs={{0,1},{1,0},{2,3},{3,2},{4,5},{5,4},{6,7},{7,6},{8,9},{9,8},{10,11... | collective-permute-start | bytes 69128 | tf_op jit(solution)/shard_map/ppermute | solution.py:340
  2.2 0.8 %collective-permute-done.after_ref.near_ref = f32[45,128]{1,0:T(8,128)S(1)} collective-permute-done((f32[45,128]{1,0:T(8,128)S(1)}, f32[45,128]{1,0:T(8,128)S(1)}, u32[]{:S(2)}, u32[]{:S(2)}) %collective-permute-start) | collective-permute-done | bytes 23072 | tf_op jit(solution)/shard_map/ppermute | solution.py:340
  3.1 4.5 %collective-permute-start.1 = (f32[36,128]{1,0:T(8,128)S(1)}, f32[36,128]{1,0:T(8,128)S(1)}, u32[]{:S(2)}, u32[]{:S(2)}) collective-permute-start(f32[36,128]{1,0:T(8,128)S(1)} %pad_maximum_fusion), channel_id=1, source_target_pairs={{0,2},{1,0},{2,4},{3,1},{4,6},{5,3},{6,8},{7,5},{8,10},{9,7},{10,1... | collective-permute-start | bytes 55304 | tf_op jit(solution)/shard_map/ppermute | solution.py:351
  7.6 0.4 collective-permute-start.2
  8.1 4.0 %collective-permute-done.2.two_ref = f32[27,128]{1,0:T(8,128)S(1)} collective-permute-done((f32[27,128]{1,0:T(8,128)S(1)}, f32[27,128]{1,0:T(8,128)S(1)}, u32[]{:S(2)}, u32[]{:S(2)}) %collective-permute-start.2) | collective-permute-done | bytes 13856 | tf_op jit(solution)/shard_map/ppermute | solution.py:351
  12.1 0.0 collective-permute-done.1.one_ref
  12.1 1.4 %collective-permute-start.3 = (f32[27,128]{1,0:T(8,128)S(1)}, f32[27,128]{1,0:T(8,128)S(1)}, u32[]{:S(2)}, u32[]{:S(2)}) collective-permute-start(f32[27,128]{1,0:T(8,128)S(1)} %pad_maximum_fusion.4), channel_id=1, source_target_pairs={{0,1},{1,0},{2,3},{3,2},{4,5},{5,4},{6,7},{7,6},{8,9},{9,8},{10,11... | collective-permute-start | bytes 41480 | tf_op jit(solution)/shard_map/ppermute | solution.py:340
  13.5 3.2 %prep.1 = (bf16[8,30,30,512]{3,2,1,0:T(8,128)(2,1)S(1)}, f32[8,120,8,128]{3,2,1,0:T(8,128)S(1)}, f32[8,10,512]{2,1,0:T(8,128)S(1)}, f32[8,10,512]{2,1,0:T(8,128)S(1)}) custom-call(s32[1,128]{1,0:T(1,128)S(1)} %get-tuple-element.18.live_ref, f32[3,5632]{1,0:T(4,128)S(1)} %get-tuple-element.21.field_ref, s32[10,4096]{1,0:T(8,128)S(1)} %get-tuple-element.22.conn_ref, ...), custom_call_target="tpu_custom_call" | custom-call | flops 20000000000 | bytes 8388608 | tf_op jit(solution)/shard_map/prep/pallas_call | solution.py:414
  16.7 0.0 collective-permute-done.3.last_ref
  16.7 0.0 copy-start
  16.8 9.3 %main.1 = (f32[66,256]{1,0:T(8,128)S(1)}, f32[36,128]{1,0:T(8,128)S(1)}, f32[18,128]{1,0:T(8,128)S(1)}, f32[18,128]{1,0:T(8,128)S(1)}) custom-call(s32[1,128]{1,0:T(1,128)S(1)} %get-tuple-element.18.live_ref, f32[45,128]{1,0:T(8,128)S(1)} %collective-permute-done.after_ref.near_ref, f32[36,128]{1,0:T(8,128)S(1)} %collective-permute-done.1.one_ref, ...), custom_call_target="tpu_custom_call" | custom-call | flops 20000000000 | bytes 8388608 | tf_op jit(solution)/shard_map/main/pallas_call | solution.py:415
  26.1 0.1 collective-permute-start.4
  26.2 1.2 %collective-permute-done.4.swap_ref = f32[36,128]{1,0:T(8,128)S(1)} collective-permute-done((f32[36,128]{1,0:T(8,128)S(1)}, f32[36,128]{1,0:T(8,128)S(1)}, u32[]{:S(2)}, u32[]{:S(2)}) %collective-permute-start.4) | collective-permute-done | bytes 18464 | tf_op jit(solution)/shard_map/ppermute | solution.py:340
  27.4 5.3 %collective-permute-start.5 = (f32[36,128]{1,0:T(8,128)S(1)}, f32[36,128]{1,0:T(8,128)S(1)}, u32[]{:S(2)}, u32[]{:S(2)}) collective-permute-start(f32[36,128]{1,0:T(8,128)S(1)} %pad_maximum_fusion.1), channel_id=1, source_target_pairs={{0,1},{1,3},{2,0},{3,5},{4,2},{5,7},{6,4},{7,9},{8,6},{9,11},{10,8... | collective-permute-start | bytes 55304 | tf_op jit(solution)/shard_map/ppermute | solution.py:351
  32.7 0.1 collective-permute-start.6
  32.7 7.1 %collective-permute-done.6.two_ref = f32[27,128]{1,0:T(8,128)S(1)} collective-permute-done((f32[27,128]{1,0:T(8,128)S(1)}, f32[27,128]{1,0:T(8,128)S(1)}, u32[]{:S(2)}, u32[]{:S(2)}) %collective-permute-start.6) | collective-permute-done | bytes 13856 | tf_op jit(solution)/shard_map/ppermute | solution.py:351
  39.8 0.0 collective-permute-done.5.one_ref
  39.9 0.1 collective-permute-start.7
  40.0 1.2 %collective-permute-done.7.last_ref = f32[36,128]{1,0:T(8,128)S(1)} collective-permute-done((f32[36,128]{1,0:T(8,128)S(1)}, f32[36,128]{1,0:T(8,128)S(1)}, u32[]{:S(2)}, u32[]{:S(2)}) %collective-permute-start.7) | collective-permute-done | bytes 18464 | tf_op jit(solution)/shard_map/ppermute | solution.py:340
  41.1 0.0 copy-done
  41.1 1.4 %spread.1 = f32[3,5632]{1,0:T(4,128)} custom-call(f32[66,256]{1,0:T(8,128)S(1)} %get-tuple-element.27.own_ref, f32[36,128]{1,0:T(8,128)S(1)} %collective-permute-done.4.swap_ref, f32[36,128]{1,0:T(8,128)S(1)} %collective-permute-done.5.one_ref, f32[27,128]{1,0:T(8,128)S(1)} %collective-permute-done.6.two_ref, f32[36,128]{1,0:T(8,128)S(1)} %collective-permute-done.7.last_ref, ...), custom_call_target="tpu_custom_call" | custom-call | tf_op jit(solution)/shard_map/spread/pallas_call | solution.py:420
  (15 shorter events, 0.1 us)
Async XLA Ops:
  1.5 1.6 %collective-permute-start = (f32[45,128]{1,0:T(8,128)S(1)}, f32[45,128]{1,0:T(8,128)S(1)}, u32[]{:S(2)}, u32[]{:S(2)}) collective-permute-start(f32[45,128]{1,0:T(8,128)S(1)} %get-tuple-element.19), channel_id=1, source_target_pairs={{0,1},{1,0},{2,3},{3,2},{4,5},{5,4},{6,7},{7,6},{8,9},{9,8},{10,11... | collective-permute-start | bytes 69128 | tf_op jit(solution)/shard_map/ppermute | solution.py:340
  3.1 9.0 %collective-permute-start.1 = (f32[36,128]{1,0:T(8,128)S(1)}, f32[36,128]{1,0:T(8,128)S(1)}, u32[]{:S(2)}, u32[]{:S(2)}) collective-permute-start(f32[36,128]{1,0:T(8,128)S(1)} %pad_maximum_fusion), channel_id=1, source_target_pairs={{0,2},{1,0},{2,4},{3,1},{4,6},{5,3},{6,8},{7,5},{8,10},{9,7},{10,1... | collective-permute-start | bytes 55304 | tf_op jit(solution)/shard_map/ppermute | solution.py:351
  7.6 4.5 %collective-permute-start.2 = (f32[27,128]{1,0:T(8,128)S(1)}, f32[27,128]{1,0:T(8,128)S(1)}, u32[]{:S(2)}, u32[]{:S(2)}) collective-permute-start(f32[27,128]{1,0:T(8,128)S(1)} %pad_maximum_fusion.3), channel_id=1, source_target_pairs={{0,4},{1,0},{2,6},{3,2},{4,8},{5,1},{6,10},{7,3},{8,12},{9,5},{10,... | collective-permute-start | bytes 41480 | tf_op jit(solution)/shard_map/ppermute | solution.py:351
  12.1 4.6 %collective-permute-start.3 = (f32[27,128]{1,0:T(8,128)S(1)}, f32[27,128]{1,0:T(8,128)S(1)}, u32[]{:S(2)}, u32[]{:S(2)}) collective-permute-start(f32[27,128]{1,0:T(8,128)S(1)} %pad_maximum_fusion.4), channel_id=1, source_target_pairs={{0,1},{1,0},{2,3},{3,2},{4,5},{5,4},{6,7},{7,6},{8,9},{9,8},{10,11... | collective-permute-start | bytes 41480 | tf_op jit(solution)/shard_map/ppermute | solution.py:340
  16.7 24.4 %copy-start = (s32[8,384]{1,0:T(8,128)S(1)}, s32[8,384]{1,0:T(8,128)}, u32[]{:S(2)}) copy-start(s32[8,384]{1,0:T(8,128)} %send_ref.1) | copy-start | bytes 36868
  26.1 1.3 %collective-permute-start.4 = (f32[36,128]{1,0:T(8,128)S(1)}, f32[36,128]{1,0:T(8,128)S(1)}, u32[]{:S(2)}, u32[]{:S(2)}) collective-permute-start(f32[36,128]{1,0:T(8,128)S(1)} %get-tuple-element.28), channel_id=1, source_target_pairs={{0,1},{1,0},{2,3},{3,2},{4,5},{5,4},{6,7},{7,6},{8,9},{9,8},{10,11... | collective-permute-start | bytes 55304 | tf_op jit(solution)/shard_map/ppermute | solution.py:340
  27.4 12.5 %collective-permute-start.5 = (f32[36,128]{1,0:T(8,128)S(1)}, f32[36,128]{1,0:T(8,128)S(1)}, u32[]{:S(2)}, u32[]{:S(2)}) collective-permute-start(f32[36,128]{1,0:T(8,128)S(1)} %pad_maximum_fusion.1), channel_id=1, source_target_pairs={{0,1},{1,3},{2,0},{3,5},{4,2},{5,7},{6,4},{7,9},{8,6},{9,11},{10,8... | collective-permute-start | bytes 55304 | tf_op jit(solution)/shard_map/ppermute | solution.py:351
  32.7 7.2 %collective-permute-start.6 = (f32[27,128]{1,0:T(8,128)S(1)}, f32[27,128]{1,0:T(8,128)S(1)}, u32[]{:S(2)}, u32[]{:S(2)}) collective-permute-start(f32[27,128]{1,0:T(8,128)S(1)} %pad_maximum_fusion.5), channel_id=1, source_target_pairs={{0,1},{1,5},{2,3},{3,7},{4,0},{5,9},{6,2},{7,11},{8,4},{9,13},{10,... | collective-permute-start | bytes 41480 | tf_op jit(solution)/shard_map/ppermute | solution.py:351
  39.9 1.3 %collective-permute-start.7 = (f32[36,128]{1,0:T(8,128)S(1)}, f32[36,128]{1,0:T(8,128)S(1)}, u32[]{:S(2)}, u32[]{:S(2)}) collective-permute-start(f32[36,128]{1,0:T(8,128)S(1)} %pad_maximum_fusion.2), channel_id=1, source_target_pairs={{0,1},{1,0},{2,3},{3,2},{4,5},{5,4},{6,7},{7,6},{8,9},{9,8},{10,11... | collective-permute-start | bytes 55304 | tf_op jit(solution)/shard_map/ppermute | solution.py:340

commit v3 on v2

--- a/solution.py
+++ b/solution.py
@@ -8,6 +8,7 @@
 
 F32 = jnp.float32
 BF16 = jnp.bfloat16
+F8 = jnp.float8_e4m3fn
 LANES = 128
 WIDE = 256
 BLK = 512
@@ -19,6 +20,8 @@
 OWN_ROWS = NODES // WIDE
 ALL_ROWS = SLOTS // WIDE
 GHOST_ROWS = ALL_ROWS - OWN_ROWS
+GHOST_PAD = 16
+OWN_PAD = 24
 TILES = BLK // LANES
 UNROLL = 2
 VMEM = pl.BlockSpec(memory_space=pltpu.VMEM)
@@ -200,7 +203,7 @@
 
 
 def main_kernel(live_ref, near_ref, one_ref, two_ref, last_ref, stiff_ref, sums_ref, lo_ref, up_ref,
-                own_ref, swap_ref, one_out_ref, two_out_ref, tf, vals, high, low, total):
+                swap_ref, one_out_ref, two_out_ref, high_ref, low_ref, tf, vals, high, low, total):
     n = own_live(live_ref)
     second = side() == 1
 
@@ -217,12 +220,12 @@
                 fill(tf, GHOST_ROWS, bundle[q:q + 1, :], c, 3 * k + j)
     table = tf[...].astype(BF16)
     total[...] = jnp.zeros_like(total)
-    lowers, uppers, parts = lower_parts(), upper_parts(ALL_ROWS), select_parts(GHOST_ROWS)
+    lowers, uppers, parts = lower_parts(), [iota_rows(16).astype(F32).astype(BF16)] * 6, select_parts(GHOST_ROWS)
 
     def gather(b, half, hots, vals):
         def chunk(a):
             cols = [pl.ds((2 * half + s) * LANES, LANES) for s in range(2)]
-            hots[a] = hot = jnp.concatenate([one_hot(lowers, lo_ref[b, pl.ds(a, 1), c]) for c in cols], axis=1).astype(jnp.float8_e4m3fn)
+            hots[a] = hot = jnp.concatenate([one_hot(lowers, lo_ref[b, pl.ds(a, 1), c]) for c in cols], axis=1).astype(F8)
             got = jnp.dot(table, hot, preferred_element_type=F32)
             for s in range(2):
                 sums = select_sums(parts, up_ref[b, pl.ds(a, 1), cols[s]] - OWN_ROWS, got, s * LANES)
@@ -242,6 +245,7 @@
         def finish():
             force = jnp.where(b < n, high[...], 0.0)
             high[...], low[...] = split(force)
+            high_ref[b, half], low_ref[b, half] = high[...], low[...]
 
         return [lambda i=i: row(i) for i in range(30)] + [finish]
 
@@ -251,8 +255,8 @@
             for s in range(2):
                 cols = pl.ds(s * LANES, LANES)
                 values = [ref[pl.ds(c * 10 + a, 1), cols] for c in range(3) for ref in (high, low)]
-                row = up_ref[b, pl.ds(a, 1), pl.ds((2 * half + s) * LANES, LANES)]
-                put.append(placed(uppers, row, values, ALL_ROWS))
+                row = up_ref[b, pl.ds(a, 1), pl.ds((2 * half + s) * LANES, LANES)] - OWN_ROWS
+                put.append(placed(uppers, row, values, GHOST_PAD))
             hot = hots[a]
             part = lax.dot_general(jnp.concatenate(put, axis=1), hot, (((1,), (1,)), ((), ())), preferred_element_type=F32)
             acc[0] = part if acc[0] is None else acc[0] + part
@@ -287,17 +291,14 @@
 
     lax.fori_loop(0, lax.div(n + (UNROLL - 1), UNROLL), step, 0)
 
-    for c in range(3):
-        base = 2 * c * ALL_ROWS
-        own_ref[pl.ds(c * OWN_ROWS, OWN_ROWS), :] = total[pl.ds(base, OWN_ROWS), :] + total[pl.ds(base + ALL_ROWS, OWN_ROWS), :]
     target = {6: (swap_ref, 0), 5: (swap_ref, 9), 7: (swap_ref, 18), 4: (swap_ref, 27),
               1: (one_out_ref, 0), 0: (one_out_ref, 9), 3: (two_out_ref, 0), 2: (two_out_ref, 9)}
 
     def partial(k, c, j):
-        h = NODES // LANES + 3 * k + j
-        at = 2 * c * ALL_ROWS + h // 2
+        h = 3 * k + j
+        at = 2 * c * GHOST_PAD + h // 2
         cols = pl.ds((h % 2) * LANES, LANES)
-        return total[pl.ds(at, 1), cols] + total[pl.ds(at + ALL_ROWS, 1), cols]
+        return total[pl.ds(at, 1), cols] + total[pl.ds(at + GHOST_PAD, 1), cols]
 
     for m in range(4):
         for c in range(3):
@@ -306,6 +307,36 @@
                 for label, x in ((m, jnp.where(second, high, low)), (m + 4, jnp.where(second, low, high))):
                     ref, base = target[label]
                     ref[pl.ds(base + c * 3 + j, 1), :] = x
+
+
+def finish_kernel(live_ref, lo_ref, up_ref, high_ref, low_ref, after_ref, own_ref, total):
+    del after_ref
+    n = own_live(live_ref)
+    lowers, uppers = lower_parts(), upper_parts(OWN_PAD)[:3] * 3
+    total[...] = jnp.zeros_like(total)
+
+    def step(trip, _):
+        acc = None
+        for k in range(UNROLL):
+            b = UNROLL * trip + k
+            for half in range(2):
+                for a in range(10):
+                    put, hot = [], []
+                    for s in range(2):
+                        inner, outer = pl.ds(s * LANES, LANES), pl.ds((2 * half + s) * LANES, LANES)
+                        hot.append(one_hot(lowers, lo_ref[b, pl.ds(a, 1), outer]))
+                        values = [ref[b, half, pl.ds(c * 10 + a, 1), inner] for c in range(3) for ref in (high_ref, low_ref)]
+                        put.append(placed(uppers, up_ref[b, pl.ds(a, 1), outer], values, OWN_PAD))
+                    part = lax.dot_general(jnp.concatenate(put, axis=1), jnp.concatenate(hot, axis=1).astype(F8),
+                                           (((1,), (1,)), ((), ())), preferred_element_type=F32)
+                    acc = part if acc is None else acc + part
+        total[...] += acc
+        return 0
+
+    lax.fori_loop(0, lax.div(n + (UNROLL - 1), UNROLL), step, 0)
+    for c in range(3):
+        base = 2 * c * OWN_PAD
+        own_ref[pl.ds(c * OWN_ROWS, OWN_ROWS), :] = total[pl.ds(base, OWN_ROWS), :] + total[pl.ds(base + OWN_PAD, OWN_ROWS), :]
 
 
 def spread_kernel(own_ref, swap_ref, one_ref, two_ref, last_ref, send_ref, out_ref, lo, up):
@@ -380,19 +411,33 @@
 def main_call():
     return pl.pallas_call(
         main_kernel,
-        out_shape=(rows_f32(3 * OWN_ROWS, WIDE), rows_f32(36, LANES), rows_f32(18, LANES), rows_f32(18, LANES)),
+        out_shape=(rows_f32(36, LANES), rows_f32(18, LANES), rows_f32(18, LANES),
+                   pltpu.VMEM((NBLK, 2, 30, BLK // 2), F32), pltpu.VMEM((NBLK, 2, 30, BLK // 2), F32)),
         in_specs=[VMEM] * 9,
-        out_specs=(VMEM,) * 4,
+        out_specs=(VMEM,) * 5,
         scratch_shapes=[
             pltpu.VMEM((table_rows(GHOST_ROWS), WIDE), F32),
             pltpu.VMEM((2 * UNROLL, 30, BLK // 2), F32),
             pltpu.VMEM((2 * UNROLL, 30, BLK // 2), F32),
             pltpu.VMEM((2 * UNROLL, 30, BLK // 2), F32),
-            pltpu.VMEM((table_rows(ALL_ROWS), WIDE), F32),
+            pltpu.VMEM((6 * GHOST_PAD, WIDE), F32),
         ],
         compiler_params=params(16384),
         cost_estimate=pl.CostEstimate(flops=2 * 10**10, bytes_accessed=2**23, transcendentals=0),
         name="main",
+    )
+
+
+def finish_call():
+    return pl.pallas_call(
+        finish_kernel,
+        out_shape=rows_f32(3 * OWN_ROWS, WIDE),
+        in_specs=[VMEM] * 6,
+        out_specs=VMEM,
+        scratch_shapes=[pltpu.VMEM((6 * OWN_PAD, WIDE), F32)],
+        compiler_params=params(12288),
+        cost_estimate=pl.CostEstimate(flops=2 * 10**10, bytes_accessed=2**23, transcendentals=0),
+        name="finish",
     )
 
 
@@ -412,10 +457,11 @@
     two = along(jnp.concatenate([out[18:], near[27:]]), 2)
     last = across(jnp.concatenate([one[18:], two[18:]]))
     stiff, sums, lo, up = prep_call()(live, field_near, conn_near, near, in_hbm(blocks))
-    own, swap, one_out, two_out = main_call()(live, near, one, two, last, stiff, sums, lo, up)
+    swap, one_out, two_out, high, low = main_call()(live, near, one, two, last, stiff, sums, lo, up)
     swapped = across(swap)
     one_in = along(jnp.concatenate([one_out, swapped[:18]]), -1)
     two_in = along(jnp.concatenate([two_out, swapped[18:27]]), -2)
+    own = finish_call()(live, lo, up, high, low, swapped)
     back = across(jnp.concatenate([one_in[9:18], one_in[27:], two_in[9:]]))
     return pl.pallas_call(
         spread_kernel,

time: 42.9 us -> 44.1 us (1.028)
  the two profiles are of different devices: /device:TPU:33 before, /device:TPU:65 now
where the time goes in v3:
time: 44.1 us; the launch traced here: 44 us
  Pallas kernels  21.9 us (50%)
  waiting for transfers between devices  13.2 us (30%)
  starting transfers between devices  8.71 us (20%)
    ppermute x4, waiting for transfers between devices, along(): return lax.ppermute(x, 'dom', list(route.items()))  11.1 us
    pallas_call x1, Pallas kernels, body(): main_call()(live, near, one, two, last, stiff, sums, lo, up)  10.8 us
    ppermute x4, starting transfers between devices, along(): return lax.ppermute(x, 'dom', list(route.items()))  6.38 us
    pallas_call x1, Pallas kernels, body(): prep_call()(live, field_near, conn_near, near, in_hbm(blocks))  4.39 us
    pallas_call x1, Pallas kernels, body(): own = finish_call()(live, lo, up, high, low, swapped)  3.9 us
    ppermute x4, starting transfers between devices, across(): lax.ppermute(x, 'dom', [(i, i ^ 1) for i in range(lax.axis_size('dom'))])  2.32 us
    ppermute x4, waiting for transfers between devices, across(): lax.ppermute(x, 'dom', [(i, i ^ 1) for i in range(lax.axis_size('dom'))])  2.03 us
    pallas_call x1, Pallas kernels, body(): pl.pallas_call(pick_kernel, out_shape=(rows_f32(45, LANES), rows_f32(27,...  1.44 us
  transfers between devices with their start and end apart: 8, of which 4 were waited for; matrix products, arithmetic and copies ran while one was open for 0% of the time, Pallas kernels for 19%

profile of v3, /device:TPU:65, one launch (start us, length us, event | category | flops | bytes accessed | tf_op | source)
XLA Modules:
  0.0 44.0 jit_solution(6812467591794893013)
XLA Ops:
  0.0 1.4 %pick.1 = (f32[45,128]{1,0:T(8,128)S(1)}, f32[27,128]{1,0:T(8,128)S(1)}, f32[3,5632]{1,0:T(4,128)S(1)}, s32[10,4096]{1,0:T(8,128)S(1)}, s32[1,128]{1,0:T(1,128)S(1)}) custom-call(f32[3,5632]{1,0:T(4,128)} %field_hbm.1, s32[8,384]{1,0:T(8,128)} %send_ref.1, s32[10,4096]{1,0:T(8,128)} %conn_hbm.1, s32[1,128]{1,0:T(1,128)} %bitcast.1), custom_call_target="tpu_custom_call" | custom-call | tf_op jit(solution)/shard_map/pick/pallas_call | solution.py:445
  1.5 0.8 %collective-permute-start = (f32[45,128]{1,0:T(8,128)S(1)}, f32[45,128]{1,0:T(8,128)S(1)}, u32[]{:S(2)}, u32[]{:S(2)}) collective-permute-start(f32[45,128]{1,0:T(8,128)S(1)} %get-tuple-element.22), channel_id=1, source_target_pairs={{0,1},{1,0},{2,3},{3,2},{4,5},{5,4},{6,7},{7,6},{8,9},{9,8},{10,11... | collective-permute-start | bytes 69128 | tf_op jit(solution)/shard_map/ppermute | solution.py:371
  2.2 0.8 %collective-permute-done.after_ref.near_ref = f32[45,128]{1,0:T(8,128)S(1)} collective-permute-done((f32[45,128]{1,0:T(8,128)S(1)}, f32[45,128]{1,0:T(8,128)S(1)}, u32[]{:S(2)}, u32[]{:S(2)}) %collective-permute-start) | collective-permute-done | bytes 23072 | tf_op jit(solution)/shard_map/ppermute | solution.py:371
  3.1 4.5 %collective-permute-start.1 = (f32[36,128]{1,0:T(8,128)S(1)}, f32[36,128]{1,0:T(8,128)S(1)}, u32[]{:S(2)}, u32[]{:S(2)}) collective-permute-start(f32[36,128]{1,0:T(8,128)S(1)} %pad_maximum_fusion), channel_id=1, source_target_pairs={{0,2},{1,0},{2,4},{3,1},{4,6},{5,3},{6,8},{7,5},{8,10},{9,7},{10,1... | collective-permute-start | bytes 55304 | tf_op jit(solution)/shard_map/ppermute | solution.py:382
  7.6 0.4 collective-permute-start.2
  8.0 4.0 %collective-permute-done.2.two_ref = f32[27,128]{1,0:T(8,128)S(1)} collective-permute-done((f32[27,128]{1,0:T(8,128)S(1)}, f32[27,128]{1,0:T(8,128)S(1)}, u32[]{:S(2)}, u32[]{:S(2)}) %collective-permute-start.2) | collective-permute-done | bytes 13856 | tf_op jit(solution)/shard_map/ppermute | solution.py:382
  12.1 0.0 collective-permute-done.1.one_ref
  12.1 1.4 %collective-permute-start.3 = (f32[27,128]{1,0:T(8,128)S(1)}, f32[27,128]{1,0:T(8,128)S(1)}, u32[]{:S(2)}, u32[]{:S(2)}) collective-permute-start(f32[27,128]{1,0:T(8,128)S(1)} %pad_maximum_fusion.4), channel_id=1, source_target_pairs={{0,1},{1,0},{2,3},{3,2},{4,5},{5,4},{6,7},{7,6},{8,9},{9,8},{10,11... | collective-permute-start | bytes 41480 | tf_op jit(solution)/shard_map/ppermute | solution.py:371
  13.5 4.4 %prep.1 = (bf16[8,30,30,512]{3,2,1,0:T(8,128)(2,1)S(1)}, f32[8,120,8,128]{3,2,1,0:T(8,128)S(1)}, f32[8,10,512]{2,1,0:T(8,128)S(1)}, f32[8,10,512]{2,1,0:T(8,128)S(1)}) custom-call(s32[1,128]{1,0:T(1,128)S(1)} %get-tuple-element.19.live_ref, f32[3,5632]{1,0:T(4,128)S(1)} %get-tuple-element.20.field_ref, s32[10,4096]{1,0:T(8,128)S(1)} %get-tuple-element.21.conn_ref, ...), custom_call_target="tpu_custom_call" | custom-call | flops 20000000000 | bytes 8388608 | tf_op jit(solution)/shard_map/prep/pallas_call | solution.py:459
  17.9 0.0 collective-permute-done.3.last_ref
  17.9 10.8 %main.1 = (f32[36,128]{1,0:T(8,128)S(1)}, f32[18,128]{1,0:T(8,128)S(1)}, f32[18,128]{1,0:T(8,128)S(1)}, f32[8,2,30,256]{3,2,1,0:T(8,128)S(1)}, f32[8,2,30,256]{3,2,1,0:T(8,128)S(1)}) custom-call(s32[1,128]{1,0:T(1,128)S(1)} %get-tuple-element.19.live_ref, f32[45,128]{1,0:T(8,128)S(1)} %collective-permute-done.after_ref.near_ref, ...), custom_call_target="tpu_custom_call" | custom-call | flops 20000000000 | bytes 8388608 | tf_op jit(solution)/shard_map/main/pallas_call | solution.py:460
  28.8 0.1 collective-permute-start.4
  28.9 1.2 %collective-permute-done.4.after_ref.swap_ref = f32[36,128]{1,0:T(8,128)S(1)} collective-permute-done((f32[36,128]{1,0:T(8,128)S(1)}, f32[36,128]{1,0:T(8,128)S(1)}, u32[]{:S(2)}, u32[]{:S(2)}) %collective-permute-start.4) | collective-permute-done | bytes 18464 | tf_op jit(solution)/shard_map/ppermute | solution.py:371
  30.1 1.4 %collective-permute-start.5 = (f32[36,128]{1,0:T(8,128)S(1)}, f32[36,128]{1,0:T(8,128)S(1)}, u32[]{:S(2)}, u32[]{:S(2)}) collective-permute-start(f32[36,128]{1,0:T(8,128)S(1)} %pad_maximum_fusion.1), channel_id=1, source_target_pairs={{0,1},{1,3},{2,0},{3,5},{4,2},{5,7},{6,4},{7,9},{8,6},{9,11},{10,8... | collective-permute-start | bytes 55304 | tf_op jit(solution)/shard_map/ppermute | solution.py:382
  31.4 0.1 collective-permute-start.6
  31.5 7.1 %collective-permute-done.6.two_ref = f32[27,128]{1,0:T(8,128)S(1)} collective-permute-done((f32[27,128]{1,0:T(8,128)S(1)}, f32[27,128]{1,0:T(8,128)S(1)}, u32[]{:S(2)}, u32[]{:S(2)}) %collective-permute-start.6) | collective-permute-done | bytes 13856 | tf_op jit(solution)/shard_map/ppermute | solution.py:382
  38.6 0.0 collective-permute-done.5.one_ref
  38.6 0.1 collective-permute-start.7
  38.7 0.0 copy-start
  38.7 3.9 %finish.1.own_ref = f32[66,256]{1,0:T(8,128)S(1)} custom-call(s32[1,128]{1,0:T(1,128)S(1)} %get-tuple-element.19.live_ref, f32[8,10,512]{2,1,0:T(8,128)S(1)} %get-tuple-element.23.lo_ref, f32[8,10,512]{2,1,0:T(8,128)S(1)} %get-tuple-element.24.up_ref, f32[8,2,30,256]{3,2,1,0:T(8,128)S(1)} %get-tuple-element.28.high_ref, ...), custom_call_target="tpu_custom_call" | custom-call | flops 20000000000 | bytes 8388608 | tf_op jit(solution)/shard_map/finish/pallas_call | solution.py:464
  42.6 0.0 collective-permute-done.7.last_ref
  42.7 0.0 copy-done
  42.7 1.4 %spread.1 = f32[3,5632]{1,0:T(4,128)} custom-call(f32[66,256]{1,0:T(8,128)S(1)} %finish.1.own_ref, f32[36,128]{1,0:T(8,128)S(1)} %collective-permute-done.4.after_ref.swap_ref, f32[36,128]{1,0:T(8,128)S(1)} %collective-permute-done.5.one_ref, f32[27,128]{1,0:T(8,128)S(1)} %collective-permute-done.6.two_ref, f32[36,128]{1,0:T(8,128)S(1)} %collective-permute-done.7.last_ref, ...), custom_call_target="tpu_custom_call" | custom-call | tf_op jit(solution)/shard_map/spread/pallas_call | solution.py:466
  (15 shorter events, 0.1 us)
Async XLA Ops:
  1.5 1.6 %collective-permute-start = (f32[45,128]{1,0:T(8,128)S(1)}, f32[45,128]{1,0:T(8,128)S(1)}, u32[]{:S(2)}, u32[]{:S(2)}) collective-permute-start(f32[45,128]{1,0:T(8,128)S(1)} %get-tuple-element.22), channel_id=1, source_target_pairs={{0,1},{1,0},{2,3},{3,2},{4,5},{5,4},{6,7},{7,6},{8,9},{9,8},{10,11... | collective-permute-start | bytes 69128 | tf_op jit(solution)/shard_map/ppermute | solution.py:371
  3.1 9.0 %collective-permute-start.1 = (f32[36,128]{1,0:T(8,128)S(1)}, f32[36,128]{1,0:T(8,128)S(1)}, u32[]{:S(2)}, u32[]{:S(2)}) collective-permute-start(f32[36,128]{1,0:T(8,128)S(1)} %pad_maximum_fusion), channel_id=1, source_target_pairs={{0,2},{1,0},{2,4},{3,1},{4,6},{5,3},{6,8},{7,5},{8,10},{9,7},{10,1... | collective-permute-start | bytes 55304 | tf_op jit(solution)/shard_map/ppermute | solution.py:382
  7.6 4.5 %collective-permute-start.2 = (f32[27,128]{1,0:T(8,128)S(1)}, f32[27,128]{1,0:T(8,128)S(1)}, u32[]{:S(2)}, u32[]{:S(2)}) collective-permute-start(f32[27,128]{1,0:T(8,128)S(1)} %pad_maximum_fusion.3), channel_id=1, source_target_pairs={{0,4},{1,0},{2,6},{3,2},{4,8},{5,1},{6,10},{7,3},{8,12},{9,5},{10,... | collective-permute-start | bytes 41480 | tf_op jit(solution)/shard_map/ppermute | solution.py:382
  12.1 5.8 %collective-permute-start.3 = (f32[27,128]{1,0:T(8,128)S(1)}, f32[27,128]{1,0:T(8,128)S(1)}, u32[]{:S(2)}, u32[]{:S(2)}) collective-permute-start(f32[27,128]{1,0:T(8,128)S(1)} %pad_maximum_fusion.4), channel_id=1, source_target_pairs={{0,1},{1,0},{2,3},{3,2},{4,5},{5,4},{6,7},{7,6},{8,9},{9,8},{10,11... | collective-permute-start | bytes 41480 | tf_op jit(solution)/shard_map/ppermute | solution.py:371
  28.8 1.3 %collective-permute-start.4 = (f32[36,128]{1,0:T(8,128)S(1)}, f32[36,128]{1,0:T(8,128)S(1)}, u32[]{:S(2)}, u32[]{:S(2)}) collective-permute-start(f32[36,128]{1,0:T(8,128)S(1)} %get-tuple-element.30), channel_id=1, source_target_pairs={{0,1},{1,0},{2,3},{3,2},{4,5},{5,4},{6,7},{7,6},{8,9},{9,8},{10,11... | collective-permute-start | bytes 55304 | tf_op jit(solution)/shard_map/ppermute | solution.py:371
  30.1 8.5 %collective-permute-start.5 = (f32[36,128]{1,0:T(8,128)S(1)}, f32[36,128]{1,0:T(8,128)S(1)}, u32[]{:S(2)}, u32[]{:S(2)}) collective-permute-start(f32[36,128]{1,0:T(8,128)S(1)} %pad_maximum_fusion.1), channel_id=1, source_target_pairs={{0,1},{1,3},{2,0},{3,5},{4,2},{5,7},{6,4},{7,9},{8,6},{9,11},{10,8... | collective-permute-start | bytes 55304 | tf_op jit(solution)/shard_map/ppermute | solution.py:382
  31.4 7.2 %collective-permute-start.6 = (f32[27,128]{1,0:T(8,128)S(1)}, f32[27,128]{1,0:T(8,128)S(1)}, u32[]{:S(2)}, u32[]{:S(2)}) collective-permute-start(f32[27,128]{1,0:T(8,128)S(1)} %pad_maximum_fusion.5), channel_id=1, source_target_pairs={{0,1},{1,5},{2,3},{3,7},{4,0},{5,9},{6,2},{7,11},{8,4},{9,13},{10,... | collective-permute-start | bytes 41480 | tf_op jit(solution)/shard_map/ppermute | solution.py:382
  38.6 4.0 %collective-permute-start.7 = (f32[36,128]{1,0:T(8,128)S(1)}, f32[36,128]{1,0:T(8,128)S(1)}, u32[]{:S(2)}, u32[]{:S(2)}) collective-permute-start(f32[36,128]{1,0:T(8,128)S(1)} %pad_maximum_fusion.2), channel_id=1, source_target_pairs={{0,1},{1,0},{2,3},{3,2},{4,5},{5,4},{6,7},{7,6},{8,9},{9,8},{10,11... | collective-permute-start | bytes 55304 | tf_op jit(solution)/shard_map/ppermute | solution.py:371
  38.7 3.9 %copy-start = (s32[8,384]{1,0:T(8,128)S(1)}, s32[8,384]{1,0:T(8,128)}, u32[]{:S(2)}) copy-start(s32[8,384]{1,0:T(8,128)} %send_ref.1) | copy-start | bytes 36868

commit v4 on v3

--- a/solution.py
+++ b/solution.py
@@ -101,6 +101,15 @@
 def split(x):
     hi = x.astype(BF16).astype(F32)
     return hi, x - hi
+
+
+def fold(ref, count):
+    for g in range(0, count, 8):
+        rows = min(8, count - g)
+        total = ref[pl.ds(8 * g, rows, stride=8), :]
+        for t in range(1, 8):
+            total = total + ref[pl.ds(8 * g + t, rows, stride=8), :]
+        yield pl.ds(g, rows), total
 
 
 def placed(uppers, row, values, rows):
@@ -203,7 +212,7 @@
 
 
 def main_kernel(live_ref, near_ref, one_ref, two_ref, last_ref, stiff_ref, sums_ref, lo_ref, up_ref,
-                swap_ref, one_out_ref, two_out_ref, high_ref, low_ref, tf, vals, high, low, total):
+                swap_ref, one_out_ref, two_out_ref, high_ref, low_ref, tf, vals, high, low, loose_vals, loose_force, total):
     n = own_live(live_ref)
     second = side() == 1
 
@@ -222,7 +231,7 @@
     total[...] = jnp.zeros_like(total)
     lowers, uppers, parts = lower_parts(), [iota_rows(16).astype(F32).astype(BF16)] * 6, select_parts(GHOST_ROWS)
 
-    def gather(b, half, hots, vals):
+    def gather(b, half, hots, vals, loose):
         def chunk(a):
             cols = [pl.ds((2 * half + s) * LANES, LANES) for s in range(2)]
             hots[a] = hot = jnp.concatenate([one_hot(lowers, lo_ref[b, pl.ds(a, 1), c]) for c in cols], axis=1).astype(F8)
@@ -231,18 +240,28 @@
                 sums = select_sums(parts, up_ref[b, pl.ds(a, 1), cols[s]] - OWN_ROWS, got, s * LANES)
                 for c in range(3):
                     both = sums[c] + sums_ref[b, (a * TILES + 2 * half + s) * 3 + c]
-                    vals[pl.ds(c * 10 + a, 1), pl.ds(s * LANES, LANES)] = jnp.sum(both, axis=0, keepdims=True)
-
-        return [lambda a=a: chunk(a) for a in range(10)]
-
-    def apply(b, half, vals, high, low):
+                    loose[s, pl.ds((c * 10 + a) * 8, 8), :] = both
+
+        def finish():
+            for s in range(2):
+                for rows, x in fold(loose.at[s], 30):
+                    vals[rows, pl.ds(s * LANES, LANES)] = x
+
+        return [lambda a=a: chunk(a) for a in range(10)] + [finish]
+
+    def apply(b, half, vals, high, low, loose):
         def row(i):
             for s in range(2):
                 cols = pl.ds(s * LANES, LANES)
                 k = stiff_ref[b, i, :, pl.ds((2 * half + s) * LANES, LANES)].astype(F32)
-                high[pl.ds(i, 1), cols] = jnp.sum(k * vals[:, cols], axis=0, keepdims=True)
+                x = k * vals[:, cols]
+                x = x[0:8] + x[8:16] + x[16:24] + jnp.concatenate([x[24:30], jnp.zeros((2, LANES), F32)], axis=0)
+                loose[s, pl.ds(8 * i, 8), :] = x
 
         def finish():
+            for s in range(2):
+                for rows, x in fold(loose.at[s], 30):
+                    high[rows, pl.ds(s * LANES, LANES)] = x
             force = jnp.where(b < n, high[...], 0.0)
             high[...], low[...] = split(force)
             high_ref[b, half], low_ref[b, half] = high[...], low[...]
@@ -282,9 +301,9 @@
             if kind == "scatter":
                 streams.append(scatter(*units[k], hots[k], h, w, acc))
             elif kind == "apply":
-                streams.append(apply(*units[k], v, h, w))
+                streams.append(apply(*units[k], v, h, w, loose_force.at[k]))
             else:
-                streams.append(gather(*units[k], hots[k], v))
+                streams.append(gather(*units[k], hots[k], v, loose_vals.at[k]))
             together(*streams)
         total[...] += acc[0]
         return 0
@@ -356,7 +375,7 @@
             put.append(placed(uppers, up[pl.ds(m, 1), cols], values, OWN_ROWS))
     total = None
     for g in range(0, 24, 2):
-        part = lax.dot_general(jnp.concatenate(put[g:g + 2], axis=1), jnp.concatenate(hot[g:g + 2], axis=1),
+        part = lax.dot_general(jnp.concatenate(put[g:g + 2], axis=1), jnp.concatenate(hot[g:g + 2], axis=1).astype(F8),
                                (((1,), (1,)), ((), ())), preferred_element_type=F32)
         total = part if total is None else total + part
     for c in range(3):
@@ -420,6 +439,8 @@
             pltpu.VMEM((2 * UNROLL, 30, BLK // 2), F32),
             pltpu.VMEM((2 * UNROLL, 30, BLK // 2), F32),
             pltpu.VMEM((2 * UNROLL, 30, BLK // 2), F32),
+            pltpu.VMEM((2 * UNROLL, 2, 240, LANES), F32),
+            pltpu.VMEM((2 * UNROLL, 2, 240, LANES), F32),
             pltpu.VMEM((6 * GHOST_PAD, WIDE), F32),
         ],
         compiler_params=params(16384),

time: 44.1 us -> 43.5 us (0.986)
  Pallas kernels: 21.9 us -> 21.3 us
where the time goes in v4:
time: 43.5 us; the launch traced here: 43.4 us
  Pallas kernels  21.3 us (49%)
  waiting for transfers between devices  13.2 us (30%)
  starting transfers between devices  8.71 us (20%)
    ppermute x4, waiting for transfers between devices, along(): return lax.ppermute(x, 'dom', list(route.items()))  11.1 us
    pallas_call x1, Pallas kernels, body(): main_call()(live, near, one, two, last, stiff, sums, lo, up)  10.5 us
    ppermute x4, starting transfers between devices, along(): return lax.ppermute(x, 'dom', list(route.items()))  6.39 us
    pallas_call x1, Pallas kernels, body(): prep_call()(live, field_near, conn_near, near, in_hbm(blocks))  4.39 us
    pallas_call x1, Pallas kernels, body(): own = finish_call()(live, lo, up, high, low, swapped)  3.9 us
    ppermute x4, starting transfers between devices, across(): lax.ppermute(x, 'dom', [(i, i ^ 1) for i in range(lax.axis_size('dom'))])  2.32 us
    ppermute x4, waiting for transfers between devices, across(): lax.ppermute(x, 'dom', [(i, i ^ 1) for i in range(lax.axis_size('dom'))])  2.03 us
    pallas_call x1, Pallas kernels, body(): pl.pallas_call(pick_kernel, out_shape=(rows_f32(45, LANES), rows_f32(27,...  1.44 us
  transfers between devices with their start and end apart: 8, of which 4 were waited for; matrix products, arithmetic and copies ran while one was open for 0% of the time, Pallas kernels for 19%

profile of v4, /device:TPU:65, one launch (start us, length us, event | category | flops | bytes accessed | tf_op | source)
XLA Modules:
  0.0 43.4 jit_solution(11932116032638824501)
XLA Ops:
  0.0 1.4 %pick.1 = (f32[45,128]{1,0:T(8,128)S(1)}, f32[27,128]{1,0:T(8,128)S(1)}, f32[3,5632]{1,0:T(4,128)S(1)}, s32[10,4096]{1,0:T(8,128)S(1)}, s32[1,128]{1,0:T(1,128)S(1)}) custom-call(f32[3,5632]{1,0:T(4,128)} %field_hbm.1, s32[8,384]{1,0:T(8,128)} %send_ref.1, s32[10,4096]{1,0:T(8,128)} %conn_hbm.1, s32[1,128]{1,0:T(1,128)} %bitcast.1), custom_call_target="tpu_custom_call" | custom-call | tf_op jit(solution)/shard_map/pick/pallas_call | solution.py:466
  1.5 0.8 %collective-permute-start = (f32[45,128]{1,0:T(8,128)S(1)}, f32[45,128]{1,0:T(8,128)S(1)}, u32[]{:S(2)}, u32[]{:S(2)}) collective-permute-start(f32[45,128]{1,0:T(8,128)S(1)} %get-tuple-element.22), channel_id=1, source_target_pairs={{0,1},{1,0},{2,3},{3,2},{4,5},{5,4},{6,7},{7,6},{8,9},{9,8},{10,11... | collective-permute-start | bytes 69128 | tf_op jit(solution)/shard_map/ppermute | solution.py:390
  2.2 0.8 %collective-permute-done.after_ref.near_ref = f32[45,128]{1,0:T(8,128)S(1)} collective-permute-done((f32[45,128]{1,0:T(8,128)S(1)}, f32[45,128]{1,0:T(8,128)S(1)}, u32[]{:S(2)}, u32[]{:S(2)}) %collective-permute-start) | collective-permute-done | bytes 23072 | tf_op jit(solution)/shard_map/ppermute | solution.py:390
  3.1 4.5 %collective-permute-start.1 = (f32[36,128]{1,0:T(8,128)S(1)}, f32[36,128]{1,0:T(8,128)S(1)}, u32[]{:S(2)}, u32[]{:S(2)}) collective-permute-start(f32[36,128]{1,0:T(8,128)S(1)} %pad_maximum_fusion), channel_id=1, source_target_pairs={{0,2},{1,0},{2,4},{3,1},{4,6},{5,3},{6,8},{7,5},{8,10},{9,7},{10,1... | collective-permute-start | bytes 55304 | tf_op jit(solution)/shard_map/ppermute | solution.py:401
  7.6 0.4 collective-permute-start.2
  8.0 4.0 %collective-permute-done.2.two_ref = f32[27,128]{1,0:T(8,128)S(1)} collective-permute-done((f32[27,128]{1,0:T(8,128)S(1)}, f32[27,128]{1,0:T(8,128)S(1)}, u32[]{:S(2)}, u32[]{:S(2)}) %collective-permute-start.2) | collective-permute-done | bytes 13856 | tf_op jit(solution)/shard_map/ppermute | solution.py:401
  12.1 0.0 collective-permute-done.1.one_ref
  12.1 1.4 %collective-permute-start.3 = (f32[27,128]{1,0:T(8,128)S(1)}, f32[27,128]{1,0:T(8,128)S(1)}, u32[]{:S(2)}, u32[]{:S(2)}) collective-permute-start(f32[27,128]{1,0:T(8,128)S(1)} %pad_maximum_fusion.4), channel_id=1, source_target_pairs={{0,1},{1,0},{2,3},{3,2},{4,5},{5,4},{6,7},{7,6},{8,9},{9,8},{10,11... | collective-permute-start | bytes 41480 | tf_op jit(solution)/shard_map/ppermute | solution.py:390
  13.5 4.4 %prep.1 = (bf16[8,30,30,512]{3,2,1,0:T(8,128)(2,1)S(1)}, f32[8,120,8,128]{3,2,1,0:T(8,128)S(1)}, f32[8,10,512]{2,1,0:T(8,128)S(1)}, f32[8,10,512]{2,1,0:T(8,128)S(1)}) custom-call(s32[1,128]{1,0:T(1,128)S(1)} %get-tuple-element.19.live_ref, f32[3,5632]{1,0:T(4,128)S(1)} %get-tuple-element.20.field_ref, s32[10,4096]{1,0:T(8,128)S(1)} %get-tuple-element.21.conn_ref, ...), custom_call_target="tpu_custom_call" | custom-call | flops 20000000000 | bytes 8388608 | tf_op jit(solution)/shard_map/prep/pallas_call | solution.py:480
  17.9 0.0 collective-permute-done.3.last_ref
  17.9 10.5 %main.1 = (f32[36,128]{1,0:T(8,128)S(1)}, f32[18,128]{1,0:T(8,128)S(1)}, f32[18,128]{1,0:T(8,128)S(1)}, f32[8,2,30,256]{3,2,1,0:T(8,128)S(1)}, f32[8,2,30,256]{3,2,1,0:T(8,128)S(1)}) custom-call(s32[1,128]{1,0:T(1,128)S(1)} %get-tuple-element.19.live_ref, f32[45,128]{1,0:T(8,128)S(1)} %collective-permute-done.after_ref.near_ref, ...), custom_call_target="tpu_custom_call" | custom-call | flops 20000000000 | bytes 8388608 | tf_op jit(solution)/shard_map/main/pallas_call | solution.py:481
  28.4 0.1 collective-permute-start.4
  28.5 1.2 %collective-permute-done.4.after_ref.swap_ref = f32[36,128]{1,0:T(8,128)S(1)} collective-permute-done((f32[36,128]{1,0:T(8,128)S(1)}, f32[36,128]{1,0:T(8,128)S(1)}, u32[]{:S(2)}, u32[]{:S(2)}) %collective-permute-start.4) | collective-permute-done | bytes 18464 | tf_op jit(solution)/shard_map/ppermute | solution.py:390
  29.7 1.4 %collective-permute-start.5 = (f32[36,128]{1,0:T(8,128)S(1)}, f32[36,128]{1,0:T(8,128)S(1)}, u32[]{:S(2)}, u32[]{:S(2)}) collective-permute-start(f32[36,128]{1,0:T(8,128)S(1)} %pad_maximum_fusion.1), channel_id=1, source_target_pairs={{0,1},{1,3},{2,0},{3,5},{4,2},{5,7},{6,4},{7,9},{8,6},{9,11},{10,8... | collective-permute-start | bytes 55304 | tf_op jit(solution)/shard_map/ppermute | solution.py:401
  31.1 0.1 collective-permute-start.6
  31.1 7.1 %collective-permute-done.6.two_ref = f32[27,128]{1,0:T(8,128)S(1)} collective-permute-done((f32[27,128]{1,0:T(8,128)S(1)}, f32[27,128]{1,0:T(8,128)S(1)}, u32[]{:S(2)}, u32[]{:S(2)}) %collective-permute-start.6) | collective-permute-done | bytes 13856 | tf_op jit(solution)/shard_map/ppermute | solution.py:401
  38.2 0.0 collective-permute-done.5.one_ref
  38.3 0.1 collective-permute-start.7
  38.4 0.0 copy-start
  38.4 3.9 %finish.1.own_ref = f32[66,256]{1,0:T(8,128)S(1)} custom-call(s32[1,128]{1,0:T(1,128)S(1)} %get-tuple-element.19.live_ref, f32[8,10,512]{2,1,0:T(8,128)S(1)} %get-tuple-element.23.lo_ref, f32[8,10,512]{2,1,0:T(8,128)S(1)} %get-tuple-element.24.up_ref, f32[8,2,30,256]{3,2,1,0:T(8,128)S(1)} %get-tuple-element.28.high_ref, ...), custom_call_target="tpu_custom_call" | custom-call | flops 20000000000 | bytes 8388608 | tf_op jit(solution)/shard_map/finish/pallas_call | solution.py:485
  42.3 0.0 collective-permute-done.7.last_ref
  42.3 0.0 copy-done
  42.3 1.1 %spread.1 = f32[3,5632]{1,0:T(4,128)} custom-call(f32[66,256]{1,0:T(8,128)S(1)} %finish.1.own_ref, f32[36,128]{1,0:T(8,128)S(1)} %collective-permute-done.4.after_ref.swap_ref, f32[36,128]{1,0:T(8,128)S(1)} %collective-permute-done.5.one_ref, f32[27,128]{1,0:T(8,128)S(1)} %collective-permute-done.6.two_ref, f32[36,128]{1,0:T(8,128)S(1)} %collective-permute-done.7.last_ref, ...), custom_call_target="tpu_custom_call" | custom-call | tf_op jit(solution)/shard_map/spread/pallas_call | solution.py:487
  (15 shorter events, 0.1 us)
Async XLA Ops:
  1.5 1.6 %collective-permute-start = (f32[45,128]{1,0:T(8,128)S(1)}, f32[45,128]{1,0:T(8,128)S(1)}, u32[]{:S(2)}, u32[]{:S(2)}) collective-permute-start(f32[45,128]{1,0:T(8,128)S(1)} %get-tuple-element.22), channel_id=1, source_target_pairs={{0,1},{1,0},{2,3},{3,2},{4,5},{5,4},{6,7},{7,6},{8,9},{9,8},{10,11... | collective-permute-start | bytes 69128 | tf_op jit(solution)/shard_map/ppermute | solution.py:390
  3.1 9.0 %collective-permute-start.1 = (f32[36,128]{1,0:T(8,128)S(1)}, f32[36,128]{1,0:T(8,128)S(1)}, u32[]{:S(2)}, u32[]{:S(2)}) collective-permute-start(f32[36,128]{1,0:T(8,128)S(1)} %pad_maximum_fusion), channel_id=1, source_target_pairs={{0,2},{1,0},{2,4},{3,1},{4,6},{5,3},{6,8},{7,5},{8,10},{9,7},{10,1... | collective-permute-start | bytes 55304 | tf_op jit(solution)/shard_map/ppermute | solution.py:401
  7.6 4.5 %collective-permute-start.2 = (f32[27,128]{1,0:T(8,128)S(1)}, f32[27,128]{1,0:T(8,128)S(1)}, u32[]{:S(2)}, u32[]{:S(2)}) collective-permute-start(f32[27,128]{1,0:T(8,128)S(1)} %pad_maximum_fusion.3), channel_id=1, source_target_pairs={{0,4},{1,0},{2,6},{3,2},{4,8},{5,1},{6,10},{7,3},{8,12},{9,5},{10,... | collective-permute-start | bytes 41480 | tf_op jit(solution)/shard_map/ppermute | solution.py:401
  12.1 5.8 %collective-permute-start.3 = (f32[27,128]{1,0:T(8,128)S(1)}, f32[27,128]{1,0:T(8,128)S(1)}, u32[]{:S(2)}, u32[]{:S(2)}) collective-permute-start(f32[27,128]{1,0:T(8,128)S(1)} %pad_maximum_fusion.4), channel_id=1, source_target_pairs={{0,1},{1,0},{2,3},{3,2},{4,5},{5,4},{6,7},{7,6},{8,9},{9,8},{10,11... | collective-permute-start | bytes 41480 | tf_op jit(solution)/shard_map/ppermute | solution.py:390
  28.4 1.3 %collective-permute-start.4 = (f32[36,128]{1,0:T(8,128)S(1)}, f32[36,128]{1,0:T(8,128)S(1)}, u32[]{:S(2)}, u32[]{:S(2)}) collective-permute-start(f32[36,128]{1,0:T(8,128)S(1)} %get-tuple-element.30), channel_id=1, source_target_pairs={{0,1},{1,0},{2,3},{3,2},{4,5},{5,4},{6,7},{7,6},{8,9},{9,8},{10,11... | collective-permute-start | bytes 55304 | tf_op jit(solution)/shard_map/ppermute | solution.py:390
  29.7 8.6 %collective-permute-start.5 = (f32[36,128]{1,0:T(8,128)S(1)}, f32[36,128]{1,0:T(8,128)S(1)}, u32[]{:S(2)}, u32[]{:S(2)}) collective-permute-start(f32[36,128]{1,0:T(8,128)S(1)} %pad_maximum_fusion.1), channel_id=1, source_target_pairs={{0,1},{1,3},{2,0},{3,5},{4,2},{5,7},{6,4},{7,9},{8,6},{9,11},{10,8... | collective-permute-start | bytes 55304 | tf_op jit(solution)/shard_map/ppermute | solution.py:401
  31.1 7.2 %collective-permute-start.6 = (f32[27,128]{1,0:T(8,128)S(1)}, f32[27,128]{1,0:T(8,128)S(1)}, u32[]{:S(2)}, u32[]{:S(2)}) collective-permute-start(f32[27,128]{1,0:T(8,128)S(1)} %pad_maximum_fusion.5), channel_id=1, source_target_pairs={{0,1},{1,5},{2,3},{3,7},{4,0},{5,9},{6,2},{7,11},{8,4},{9,13},{10,... | collective-permute-start | bytes 41480 | tf_op jit(solution)/shard_map/ppermute | solution.py:401
  38.3 4.0 %collective-permute-start.7 = (f32[36,128]{1,0:T(8,128)S(1)}, f32[36,128]{1,0:T(8,128)S(1)}, u32[]{:S(2)}, u32[]{:S(2)}) collective-permute-start(f32[36,128]{1,0:T(8,128)S(1)} %pad_maximum_fusion.2), channel_id=1, source_target_pairs={{0,1},{1,0},{2,3},{3,2},{4,5},{5,4},{6,7},{7,6},{8,9},{9,8},{10,11... | collective-permute-start | bytes 55304 | tf_op jit(solution)/shard_map/ppermute | solution.py:390
  38.4 3.9 %copy-start = (s32[8,384]{1,0:T(8,128)S(1)}, s32[8,384]{1,0:T(8,128)}, u32[]{:S(2)}) copy-start(s32[8,384]{1,0:T(8,128)} %send_ref.1) | copy-start | bytes 36868
